TPU v7x, 32 devices: a whole 2x2x4 slice. The times are simulated.
32 devices in a mesh: dp: 4 (over x, core), seq: 8 (over z, y).
Axes of the slice: x: 2, y: 2, z: 4, core: 2. Of those that a mesh axis runs over, the one named last changes fastest.
Arguments:
- frames: float32 [32, 768, 512], P('dp', 'seq'), may hold values from -6 to 6
- lengths: int32 [32], replicated, may hold values from 192 to 768, as said below
- cotangent: float32 [32, 768, 512], P('dp', 'seq'), may hold values from -6 to 6
- gains: bfloat16 [1, 6, 512], P(None, None, ('dp', 'seq')), may hold values from 0.5 to 1.5
- shifts: bfloat16 [1, 6, 512], P(None, None, ('dp', 'seq')), may hold values from -3 to 3
- rel_bias: bfloat16 [1, 2, 512], P(None, None, ('dp', 'seq')), may hold values from -3 to 3
- ffn_up: bfloat16 [1, 2, 512, 2048], P(None, None, ('dp', 'seq')), may hold values from -0.25 to 0.25
- ffn_down: bfloat16 [1, 2, 2048, 512], P(None, None, ('dp', 'seq')), may hold values from -0.125 to 0.125
- attn_in: bfloat16 [1, 512, 1536], P(None, ('dp', 'seq')), may hold values from -1 to 1
- attn_out: bfloat16 [1, 512, 512], P(None, ('dp', 'seq')), may hold values from -1 to 1
- pos_proj: bfloat16 [1, 512, 512], P(None, ('dp', 'seq')), may hold values from -0.25 to 0.25
- conv_in: bfloat16 [1, 512, 1024], P(None, ('dp', 'seq')), may hold values from -0.25 to 0.25
- depthwise: bfloat16 [1, 512, 31], P(None, ('dp', 'seq')), may hold values from -1 to 1
- conv_out: bfloat16 [1, 512, 512], P(None, ('dp', 'seq')), may hold values from -0.25 to 0.25
Outputs:
- mixed: float32 [32, 768, 512], P('dp', 'seq')
- grad_frames: float32 [32, 768, 512], P('dp', 'seq')
- grad_gains: float32 [1, 6, 512], P(None, None, ('dp', 'seq'))
- grad_shifts: float32 [1, 6, 512], P(None, None, ('dp', 'seq'))
- grad_rel_bias: float32 [1, 2, 512], P(None, None, ('dp', 'seq'))
- grad_ffn_up: float32 [1, 2, 512, 2048], P(None, None, ('dp', 'seq'))
- grad_ffn_down: float32 [1, 2, 2048, 512], P(None, None, ('dp', 'seq'))
- grad_attn_in: float32 [1, 512, 1536], P(None, ('dp', 'seq'))
- grad_attn_out: float32 [1, 512, 512], P(None, ('dp', 'seq'))
- grad_pos_proj: float32 [1, 512, 512], P(None, ('dp', 'seq'))
- grad_conv_in: float32 [1, 512, 1024], P(None, ('dp', 'seq'))
- grad_depthwise: float32 [1, 512, 31], P(None, ('dp', 'seq'))
- grad_conv_out: float32 [1, 512, 512], P(None, ('dp', 'seq'))
Inputs may be any that keep to these rules, and one draw needn't show every extreme that they name: `lengths`: some utterance has exactly 768 valid frames and some exactly 192.
All inputs are finite; a program needn't handle non-finite values.
Results may differ from a plain program's by a relative error of at most 0.019.
Values may be sent and summed in bfloat16 or wider, within the bound.
A program may use at most 384 MiB of HBM per device.

v0:
```python
import math

import jax
import jax.numpy as jnp
import numpy as np
from jax import lax
from jax.experimental import pallas as pl
from jax.experimental.pallas import tpu as pltpu
from jax.sharding import PartitionSpec as P

H = 8
DH = 64
NL = 1
MB = 2


HIGHEST_PREC = lax.Precision.HIGHEST


def extended(cells, sides, width):
    for axis, dim in sides:
        count = lax.axis_size(axis)
        ends = count - 1
        head = lax.slice_in_dim(cells, 0, width, axis=dim)
        tail = lax.slice_in_dim(cells, cells.shape[dim] - width, cells.shape[dim], axis=dim)
        cells = jnp.concatenate(
            [
                lax.ppermute(tail, axis, [(i, (i + 1) % count) for i in range(ends)]),
                cells,
                lax.ppermute(head, axis, [((i + 1) % count, i) for i in range(ends)]),
            ],
            axis=dim,
        )
    return cells


def layer_norm(values, gain_row, shift_row):
    centred = values - jnp.mean(values, axis=-1, keepdims=True)
    spread = jnp.mean(centred * centred, axis=-1, keepdims=True)
    return centred * lax.rsqrt(spread + 1e-05) * gain_row + shift_row


def sinusoid(offsets, model_width):
    half_width = model_width // 2
    frequency = jnp.exp(
        jnp.arange(half_width, dtype=jnp.float32) * (-2.0 * math.log(10000.0) / model_width)
    )
    angles = offsets.astype(jnp.float32)[:, None] * frequency[None, :]
    return jnp.concatenate([jnp.sin(angles), jnp.cos(angles)], axis=1)


def skew_rows(raw_pos, key_count):
    row_count = raw_pos.shape[-2]
    col_count = raw_pos.shape[-1]
    lead = raw_pos.shape[:-2]
    flat_rows = raw_pos.reshape(lead + (row_count * col_count,))
    flat_rows = flat_rows[..., row_count - 1 : row_count - 1 + row_count * (col_count - 1)]
    return flat_rows.reshape(lead + (row_count, col_count - 1))[..., :key_count]


def skew_back(grad_skew, raw_shape, key_count):
    zero_raw = jnp.zeros(raw_shape, jnp.float32)
    return jax.vjp(lambda raw_pos: skew_rows(raw_pos, key_count), zero_raw)[1](grad_skew)[0]


def glu_gate(gate_pair):
    half_width = gate_pair.shape[-1] // 2
    return gate_pair[..., :half_width] * jax.nn.sigmoid(gate_pair[..., half_width:])


def matmul_low(left, right):
    return jnp.dot(left, right, preferred_element_type=jnp.float32)


def matmul_back(grad_low, weight):
    return lax.dot_general(
        grad_low, weight, (((1,), (1,)), ((), ())), preferred_element_type=jnp.float32
    )


def weight_grad(inputs_low, grad_low):
    return lax.dot_general(
        inputs_low, grad_low, (((0,), (0,)), ((), ())), preferred_element_type=jnp.float32
    )


def ffn_forward(row_data, gain_row, shift_row, w_up, w_down):
    normed_b = layer_norm(row_data, gain_row, shift_row).astype(jnp.bfloat16)
    hidden = matmul_low(normed_b, w_up)
    active_b = jax.nn.silu(hidden).astype(jnp.bfloat16)
    branch = matmul_low(active_b, w_down)
    return (row_data + 0.5 * branch, (row_data, normed_b, hidden, active_b))


def ffn_backward(grad_rows, kept_data, gain_row, shift_row, w_up, w_down):
    row_data, normed_b, hidden, active_b = kept_data
    grad_out_b = (0.5 * grad_rows).astype(jnp.bfloat16)
    g_down = weight_grad(active_b, grad_out_b)
    grad_active = matmul_back(grad_out_b, w_down)
    grad_hidden_b = jax.vjp(jax.nn.silu, hidden)[1](grad_active)[0].astype(jnp.bfloat16)
    g_up = weight_grad(normed_b, grad_hidden_b)
    grad_normed = matmul_back(grad_hidden_b, w_up)
    grad_ln, g_gain, g_shift = jax.vjp(layer_norm, row_data, gain_row, shift_row)[1](grad_normed)
    return (grad_rows + grad_ln, (g_gain, g_shift, g_up, g_down))


def attention_logits(query_u_b, query_v_b, key_heads, pos_heads, key_valid):
    content = jnp.einsum(
        "ufhd,ulhd->uhfl", query_u_b, key_heads, preferred_element_type=jnp.float32
    )
    raw_pos = jnp.einsum("ufhd,whd->uhfw", query_v_b, pos_heads, preferred_element_type=jnp.float32)
    logits = (content + skew_rows(raw_pos, key_heads.shape[1])) * 0.125
    return jnp.where(key_valid[:, None, None, :], logits, -1e30)


def attn_forward(
    row_data,
    utt_count,
    gain_row,
    shift_row,
    bias_u,
    bias_v,
    w_in,
    w_out,
    w_pos,
    key_valid,
    pos_table_b,
):
    model_width = row_data.shape[1]
    frame_len = row_data.shape[0] // utt_count
    normed_b = layer_norm(row_data, gain_row, shift_row).astype(jnp.bfloat16)
    proj_rows = matmul_low(normed_b, w_in)
    query_rows = proj_rows[:, :model_width].reshape(utt_count, frame_len, H, DH)
    key_b = (
        proj_rows[:, model_width : 2 * model_width]
        .astype(jnp.bfloat16)
        .reshape(utt_count, frame_len, model_width)
    )
    value_b = (
        proj_rows[:, 2 * model_width :]
        .astype(jnp.bfloat16)
        .reshape(utt_count, frame_len, model_width)
    )
    all_keys, all_values = (
        lax.all_gather(key_b, "seq", axis=1, tiled=True),
        lax.all_gather(value_b, "seq", axis=1, tiled=True),
    )
    key_heads = all_keys.reshape(utt_count, -1, H, DH)
    value_heads = all_values.reshape(utt_count, -1, H, DH)
    query_u_b = (query_rows + bias_u.reshape(H, DH)).astype(jnp.bfloat16)
    query_v_b = (query_rows + bias_v.reshape(H, DH)).astype(jnp.bfloat16)
    pos_heads = matmul_low(pos_table_b, w_pos).astype(jnp.bfloat16).reshape(-1, H, DH)
    logits = attention_logits(query_u_b, query_v_b, key_heads, pos_heads, key_valid)
    top_score = jnp.max(logits, axis=-1, keepdims=True)
    exp_scores = jnp.exp(logits - top_score)
    row_total = jnp.sum(exp_scores, axis=-1, keepdims=True)
    prob_b = (exp_scores / row_total).astype(jnp.bfloat16)
    log_total = top_score + jnp.log(row_total)
    context = jnp.einsum("uhfl,ulhd->ufhd", prob_b, value_heads, preferred_element_type=jnp.float32)
    context_b = context.astype(jnp.bfloat16).reshape(-1, model_width)
    branch = matmul_low(context_b, w_out)
    kept_data = (
        row_data,
        normed_b,
        query_u_b,
        query_v_b,
        key_heads,
        value_heads,
        pos_heads,
        log_total,
        context_b,
    )
    return (row_data + branch, kept_data)


def attn_backward(grad_rows, kept_data, gain_row, shift_row, w_in, w_out, key_valid, pos_table_b):
    (
        row_data,
        normed_b,
        query_u_b,
        query_v_b,
        key_heads,
        value_heads,
        pos_heads,
        log_total,
        context_b,
    ) = kept_data
    utt_count = query_u_b.shape[0]
    frame_len = query_u_b.shape[1]
    model_width = row_data.shape[1]
    key_len = key_heads.shape[1]
    grad_out_b = grad_rows.astype(jnp.bfloat16)
    g_out = weight_grad(context_b, grad_out_b)
    grad_context_b = (
        matmul_back(grad_out_b, w_out).astype(jnp.bfloat16).reshape(utt_count, frame_len, H, DH)
    )
    logits = attention_logits(query_u_b, query_v_b, key_heads, pos_heads, key_valid)
    prob_rows = jnp.exp(logits - log_total)
    grad_probs = jnp.einsum(
        "ufhd,ulhd->uhfl", grad_context_b, value_heads, preferred_element_type=jnp.float32
    )
    inner_sum = jnp.sum(grad_probs * prob_rows, axis=-1, keepdims=True)
    grad_logits_b = (prob_rows * (grad_probs - inner_sum)).astype(jnp.bfloat16) * 0.125
    grad_query_u = jnp.einsum(
        "uhfl,ulhd->ufhd", grad_logits_b, key_heads, preferred_element_type=jnp.float32
    )
    raw_shape = (utt_count, H, frame_len, pos_heads.shape[0])
    grad_raw_b = skew_back(grad_logits_b.astype(jnp.float32), raw_shape, key_len).astype(
        jnp.bfloat16
    )
    grad_query_v = jnp.einsum(
        "uhfw,whd->ufhd", grad_raw_b, pos_heads, preferred_element_type=jnp.float32
    )
    grad_pos = jnp.einsum(
        "uhfw,ufhd->whd", grad_raw_b, query_v_b, preferred_element_type=jnp.float32
    )
    grad_pos = grad_pos.reshape(-1, model_width)
    g_pos = lax.dot_general(
        pos_table_b.astype(jnp.float32),
        grad_pos,
        (((0,), (0,)), ((), ())),
        precision=HIGHEST_PREC,
        preferred_element_type=jnp.float32,
    )
    prob_b = prob_rows.astype(jnp.bfloat16)
    grad_values = jnp.einsum(
        "uhfl,ufhd->ulhd", prob_b, grad_context_b, preferred_element_type=jnp.float32
    )
    grad_keys = jnp.einsum(
        "uhfl,ufhd->ulhd", grad_logits_b, query_u_b, preferred_element_type=jnp.float32
    )
    own_keys, own_values = (
        lax.psum_scatter(
            grad_keys.reshape(utt_count, key_len, model_width),
            "seq",
            scatter_dimension=1,
            tiled=True,
        ),
        lax.psum_scatter(
            grad_values.reshape(utt_count, key_len, model_width),
            "seq",
            scatter_dimension=1,
            tiled=True,
        ),
    )
    g_bias_u = jnp.sum(grad_query_u, axis=(0, 1)).reshape(-1)
    g_bias_v = jnp.sum(grad_query_v, axis=(0, 1)).reshape(-1)
    grad_proj_b = jnp.concatenate(
        [
            (grad_query_u + grad_query_v).reshape(-1, model_width),
            own_keys.reshape(-1, model_width),
            own_values.reshape(-1, model_width),
        ],
        axis=1,
    ).astype(jnp.bfloat16)
    g_in = weight_grad(normed_b, grad_proj_b)
    grad_normed = matmul_back(grad_proj_b, w_in)
    grad_ln, g_gain, g_shift = jax.vjp(layer_norm, row_data, gain_row, shift_row)[1](grad_normed)
    return (grad_rows + grad_ln, (g_gain, g_shift, g_bias_u, g_bias_v, g_in, g_out, g_pos))


def conv_forward(
    row_data,
    utt_count,
    gain_row,
    shift_row,
    w_in,
    kernel,
    bn_gain,
    bn_shift,
    w_out,
    frame_mask,
    frame_count,
):
    model_width = row_data.shape[1]
    frame_len = row_data.shape[0] // utt_count
    normed_b = layer_norm(row_data, gain_row, shift_row).astype(jnp.bfloat16)
    gate_pair = matmul_low(normed_b, w_in)
    mask_rows = frame_mask.reshape(-1, 1)
    gated_b = (
        (glu_gate(gate_pair) * mask_rows)
        .astype(jnp.bfloat16)
        .reshape(utt_count, frame_len, model_width)
    )
    halo_reach = (kernel.shape[1] - 1) // 2
    padded = extended(gated_b, (("seq", 1),), halo_reach)
    kernel_f = kernel.astype(jnp.float32)
    depth_out = padded[:, 0:frame_len].astype(jnp.float32) * kernel_f[:, 0]
    for tap_idx in range(1, kernel.shape[1]):
        depth_out = (
            depth_out
            + padded[:, tap_idx : tap_idx + frame_len].astype(jnp.float32) * kernel_f[:, tap_idx]
        )
    weight_mask = frame_mask[:, :, None]
    sum_local = jnp.sum(depth_out * weight_mask, axis=(0, 1))
    square_local = jnp.sum(depth_out * depth_out * weight_mask, axis=(0, 1))
    sum_all, square_all = lax.psum((sum_local, square_local), ("dp", "seq"))
    mean_val = sum_all / frame_count
    variance = square_all / frame_count - mean_val * mean_val
    inv_std = lax.rsqrt(variance + 1e-05)
    normal = (depth_out - mean_val) * inv_std * bn_gain + bn_shift
    active_b = jax.nn.silu(normal).astype(jnp.bfloat16).reshape(-1, model_width)
    branch = matmul_low(active_b, w_out)
    kept_data = (
        row_data,
        normed_b,
        gate_pair,
        padded,
        depth_out,
        mean_val,
        inv_std,
        normal,
        active_b,
    )
    return (row_data + branch, kept_data)


def conv_backward(
    grad_rows, kept_data, gain_row, shift_row, w_in, kernel, bn_gain, w_out, frame_mask, frame_count
):
    row_data, normed_b, gate_pair, padded, depth_out, mean_val, inv_std, normal, active_b = (
        kept_data
    )
    frame_len = depth_out.shape[1]
    model_width = depth_out.shape[2]
    grad_out_b = grad_rows.astype(jnp.bfloat16)
    g_out = weight_grad(active_b, grad_out_b)
    grad_active = matmul_back(grad_out_b, w_out).reshape(depth_out.shape)
    grad_normal = jax.vjp(jax.nn.silu, normal)[1](grad_active)[0]
    centred_hat = (depth_out - mean_val) * inv_std
    g_bn_gain = jnp.sum(grad_normal * centred_hat, axis=(0, 1))
    g_bn_shift = jnp.sum(grad_normal, axis=(0, 1))
    grad_hat = grad_normal * bn_gain
    part_one = jnp.sum(grad_hat, axis=(0, 1))
    part_two = jnp.sum(grad_hat * depth_out, axis=(0, 1))
    part_one, part_two = lax.psum((part_one, part_two), ("dp", "seq"))
    grad_inv = part_two - mean_val * part_one
    grad_var = -0.5 * inv_std * inv_std * inv_std * grad_inv
    grad_mean = -inv_std * part_one - 2.0 * mean_val * grad_var
    weight_mask = frame_mask[:, :, None]
    grad_depth_b = (
        grad_hat * inv_std
        + weight_mask * (grad_mean / frame_count + 2.0 * depth_out * grad_var / frame_count)
    ).astype(jnp.bfloat16)
    halo_reach = (kernel.shape[1] - 1) // 2
    grad_padded = extended(grad_depth_b, (("seq", 1),), halo_reach)
    kernel_f = kernel.astype(jnp.float32)
    grad_depth_f = grad_depth_b.astype(jnp.float32)
    grad_gated = jnp.zeros(depth_out.shape, jnp.float32)
    kernel_cols = []
    for tap_idx in range(kernel.shape[1]):
        begin_at = 2 * halo_reach - tap_idx
        grad_gated = (
            grad_gated
            + grad_padded[:, begin_at : begin_at + frame_len].astype(jnp.float32)
            * kernel_f[:, tap_idx]
        )
        kernel_cols.append(
            jnp.sum(
                padded[:, tap_idx : tap_idx + frame_len].astype(jnp.float32) * grad_depth_f,
                axis=(0, 1),
            )
        )
    g_kernel = jnp.stack(kernel_cols, axis=1)
    grad_gate_b = jax.vjp(glu_gate, gate_pair)[1](
        (grad_gated * weight_mask).reshape(-1, model_width)
    )[0]
    grad_gate_b = grad_gate_b.astype(jnp.bfloat16)
    g_in = weight_grad(normed_b, grad_gate_b)
    grad_normed = matmul_back(grad_gate_b, w_in)
    grad_ln, g_gain, g_shift = jax.vjp(layer_norm, row_data, gain_row, shift_row)[1](grad_normed)
    return (grad_rows + grad_ln, (g_gain, g_shift, g_in, g_kernel, g_bn_gain, g_bn_shift, g_out))


def layer_forward(values, weights, frame_mask, key_valid, frame_count, pos_table_b):
    (
        gain_set,
        shift_set,
        rel_set,
        up_pair,
        down_pair,
        attn_in_w,
        attn_out_w,
        pos_w,
        conv_in_w,
        kernel,
        conv_out_w,
    ) = weights
    gain_f = gain_set.astype(jnp.float32)
    shift_f = shift_set.astype(jnp.float32)
    rel_f = rel_set.astype(jnp.float32)
    utt_count = values.shape[0]
    row_data = values.reshape(-1, values.shape[2])
    row_data, kept_one = ffn_forward(row_data, gain_f[0], shift_f[0], up_pair[0], down_pair[0])
    row_data, kept_attn = attn_forward(
        row_data,
        utt_count,
        gain_f[1],
        shift_f[1],
        rel_f[0],
        rel_f[1],
        attn_in_w,
        attn_out_w,
        pos_w,
        key_valid,
        pos_table_b,
    )
    row_data, kept_conv = conv_forward(
        row_data,
        utt_count,
        gain_f[2],
        shift_f[2],
        conv_in_w,
        kernel,
        gain_f[5],
        shift_f[5],
        conv_out_w,
        frame_mask,
        frame_count,
    )
    row_data, kept_two = ffn_forward(row_data, gain_f[3], shift_f[3], up_pair[1], down_pair[1])
    result = layer_norm(row_data, gain_f[4], shift_f[4])
    return (result.reshape(values.shape), (kept_one, kept_attn, kept_conv, kept_two, row_data))


def layer_backward(
    grad_values, kept_data, weights, frame_mask, key_valid, frame_count, pos_table_b
):
    (
        gain_set,
        shift_set,
        rel_set,
        up_pair,
        down_pair,
        attn_in_w,
        attn_out_w,
        pos_w,
        conv_in_w,
        kernel,
        conv_out_w,
    ) = weights
    gain_f = gain_set.astype(jnp.float32)
    shift_f = shift_set.astype(jnp.float32)
    kept_one, kept_attn, kept_conv, kept_two, last_rows = kept_data
    grad_rows = grad_values.reshape(-1, grad_values.shape[2])
    grad_rows, g_gain_last, g_shift_last = jax.vjp(layer_norm, last_rows, gain_f[4], shift_f[4])[1](
        grad_rows
    )
    grad_rows, two_grads = ffn_backward(
        grad_rows, kept_two, gain_f[3], shift_f[3], up_pair[1], down_pair[1]
    )
    grad_rows, conv_grads = conv_backward(
        grad_rows,
        kept_conv,
        gain_f[2],
        shift_f[2],
        conv_in_w,
        kernel,
        gain_f[5],
        conv_out_w,
        frame_mask,
        frame_count,
    )
    grad_rows, attn_grads = attn_backward(
        grad_rows, kept_attn, gain_f[1], shift_f[1], attn_in_w, attn_out_w, key_valid, pos_table_b
    )
    grad_rows, one_grads = ffn_backward(
        grad_rows, kept_one, gain_f[0], shift_f[0], up_pair[0], down_pair[0]
    )
    grad_gains = jnp.stack(
        [one_grads[0], attn_grads[0], conv_grads[0], two_grads[0], g_gain_last, conv_grads[4]]
    )
    grad_shifts = jnp.stack(
        [one_grads[1], attn_grads[1], conv_grads[1], two_grads[1], g_shift_last, conv_grads[5]]
    )
    grad_rel = jnp.stack([attn_grads[2], attn_grads[3]])
    grad_up = jnp.stack([one_grads[2], two_grads[2]])
    grad_down = jnp.stack([one_grads[3], two_grads[3]])
    layer_grads = (
        grad_gains,
        grad_shifts,
        grad_rel,
        grad_up,
        grad_down,
        attn_grads[4],
        attn_grads[5],
        attn_grads[6],
        conv_grads[2],
        conv_grads[3],
        conv_grads[6],
    )
    return (grad_rows.reshape(grad_values.shape), layer_grads)


def gather_forward(shards, layer_idx):
    pieces = tuple((member[layer_idx] for member in shards))
    return (
        lax.all_gather(pieces[0], ("dp", "seq"), axis=1, tiled=True),
        lax.all_gather(pieces[1], ("dp", "seq"), axis=1, tiled=True),
        lax.all_gather(pieces[2], ("dp", "seq"), axis=1, tiled=True),
        lax.all_gather(pieces[3], ("dp", "seq"), axis=1, tiled=True),
        lax.all_gather(pieces[4], ("dp", "seq"), axis=1, tiled=True),
        lax.all_gather(pieces[5], ("dp", "seq"), axis=0, tiled=True),
        lax.all_gather(pieces[6], ("dp", "seq"), axis=0, tiled=True),
        lax.all_gather(pieces[7], ("dp", "seq"), axis=0, tiled=True),
        lax.all_gather(pieces[8], ("dp", "seq"), axis=0, tiled=True),
        lax.all_gather(pieces[9], ("dp", "seq"), axis=0, tiled=True),
        lax.all_gather(pieces[10], ("dp", "seq"), axis=0, tiled=True),
    )


def gather_backward(shards, layer_idx):
    pieces = tuple((member[layer_idx] for member in shards))
    return (
        lax.all_gather(pieces[0], ("dp", "seq"), axis=1, tiled=True),
        lax.all_gather(pieces[1], ("dp", "seq"), axis=1, tiled=True),
        lax.all_gather(pieces[2], ("dp", "seq"), axis=1, tiled=True),
        lax.all_gather(pieces[3], ("dp", "seq"), axis=1, tiled=True),
        lax.all_gather(pieces[4], ("dp", "seq"), axis=1, tiled=True),
        lax.all_gather(pieces[5], ("dp", "seq"), axis=0, tiled=True),
        lax.all_gather(pieces[6], ("dp", "seq"), axis=0, tiled=True),
        lax.all_gather(pieces[7], ("dp", "seq"), axis=0, tiled=True),
        lax.all_gather(pieces[8], ("dp", "seq"), axis=0, tiled=True),
        lax.all_gather(pieces[9], ("dp", "seq"), axis=0, tiled=True),
        lax.all_gather(pieces[10], ("dp", "seq"), axis=0, tiled=True),
    )


def local_general(
    frames,
    lengths,
    cotangent,
    gains,
    shifts,
    rel_bias,
    ffn_up,
    ffn_down,
    attn_in,
    attn_out,
    pos_proj,
    conv_in,
    depthwise,
    conv_out,
):
    shards = (
        gains,
        shifts,
        rel_bias,
        ffn_up,
        ffn_down,
        attn_in,
        attn_out,
        pos_proj,
        conv_in,
        depthwise,
        conv_out,
    )
    groups = lax.axis_size("dp")
    seq_devices = lax.axis_size("seq")
    local_utts = frames.shape[0]
    frame_len = frames.shape[1]
    model_width = frames.shape[2]
    utt_per = local_utts // MB
    length = frame_len * seq_devices
    seq_start = lax.axis_index("seq") * frame_len
    first_utt = lax.axis_index("dp") * local_utts
    own_lengths = lax.dynamic_slice_in_dim(lengths, first_utt, local_utts)
    lengths_grid = lengths.reshape(groups, MB, utt_per)
    offsets = seq_start + frame_len - 1 - jnp.arange(length + frame_len - 1, dtype=jnp.int32)
    pos_table_b = sinusoid(offsets, model_width).astype(jnp.bfloat16)
    frame_pos = seq_start + jnp.arange(frame_len, dtype=jnp.int32)
    key_pos = jnp.arange(length, dtype=jnp.int32)
    result_list = []
    grad_list = []
    full_sums = [None] * NL
    for micro_idx in range(MB):
        lens_here = own_lengths[micro_idx * utt_per : (micro_idx + 1) * utt_per]
        frame_mask = (frame_pos[None, :] < lens_here[:, None]).astype(jnp.float32)
        key_valid = key_pos[None, :] < lens_here[:, None]
        frame_count = jnp.sum(lengths_grid[:, micro_idx]).astype(jnp.float32)
        values = frames[micro_idx * utt_per : (micro_idx + 1) * utt_per]
        held_weights = []
        layer_idx = 0
        weights = gather_forward(shards, layer_idx)
        values, kept_data = layer_forward(
            values, weights, frame_mask, key_valid, frame_count, pos_table_b
        )
        saved_acts = [kept_data]
        held_weights.append(weights)
        result_list.append(values)
        grad_values = cotangent[micro_idx * utt_per : (micro_idx + 1) * utt_per]
        for layer_idx in reversed(range(NL)):
            weights = gather_backward(shards, layer_idx)
            grad_values, layer_grads = layer_backward(
                grad_values,
                saved_acts[layer_idx],
                weights,
                frame_mask,
                key_valid,
                frame_count,
                pos_table_b,
            )
            if full_sums[layer_idx] is None:
                full_sums[layer_idx] = layer_grads
            else:
                full_sums[layer_idx] = jax.tree.map(jnp.add, full_sums[layer_idx], layer_grads)
        grad_list.append(grad_values)
    stacked = tuple((jnp.stack([full_sums[0][member]]) for member in range(11)))
    final_grads = (
        lax.psum_scatter(stacked[0], ("dp", "seq"), scatter_dimension=2, tiled=True),
        lax.psum_scatter(stacked[1], ("dp", "seq"), scatter_dimension=2, tiled=True),
        lax.psum_scatter(stacked[2], ("dp", "seq"), scatter_dimension=2, tiled=True),
        lax.psum_scatter(stacked[3], ("dp", "seq"), scatter_dimension=2, tiled=True),
        lax.psum_scatter(stacked[4], ("dp", "seq"), scatter_dimension=2, tiled=True),
        lax.psum_scatter(stacked[5], ("dp", "seq"), scatter_dimension=1, tiled=True),
        lax.psum_scatter(stacked[6], ("dp", "seq"), scatter_dimension=1, tiled=True),
        lax.psum_scatter(stacked[7], ("dp", "seq"), scatter_dimension=1, tiled=True),
        lax.psum_scatter(stacked[8], ("dp", "seq"), scatter_dimension=1, tiled=True),
        lax.psum_scatter(stacked[9], ("dp", "seq"), scatter_dimension=1, tiled=True),
        lax.psum_scatter(stacked[10], ("dp", "seq"), scatter_dimension=1, tiled=True),
    )
    mixed = jnp.concatenate(result_list, axis=0)
    grad_frames = jnp.concatenate(grad_list, axis=0)
    return (
        mixed,
        grad_frames,
        final_grads[0],
        final_grads[1],
        final_grads[2],
        final_grads[3],
        final_grads[4],
        final_grads[5],
        final_grads[6],
        final_grads[7],
        final_grads[8],
        final_grads[9],
        final_grads[10],
    )


NT = (((1,), (1,)), ((), ()))
TN = (((0,), (0,)), ((), ()))
NN = (((1,), (0,)), ((), ()))
MESH = pl.DeviceIdType.MESH
UTTS = 4
SMALL = 128
STRIP = 64
VMEM_LIMIT = 60 * 1024 * 1024


def fits_whole(mesh):
    return mesh.shape["dp"] == 4 and mesh.shape["seq"] == MB * UTTS


def dotf(left, right, dims=NN):
    return lax.dot_general(left, right, dims, preferred_element_type=jnp.float32)


def place():
    dp = lax.axis_index("dp")
    sq = lax.axis_index("seq")
    return dp, sq, lax.div(dp, 2), lax.rem(dp, 2), lax.div(sq, 2), lax.rem(sq, 2)


def flip_if(value, bit):
    return 1 - value if bit else value


def partners():
    dp, sq, x, c, z, y = place()
    even = c == 0
    core = (x * 2 + 1 - c, sq)
    xdev = ((1 - x) * 2 + c, sq)
    ydev = (dp, z * 2 + 1 - y)
    first = (jnp.where(even, ydev[0], xdev[0]), jnp.where(even, ydev[1], xdev[1]))
    second = (jnp.where(even, xdev[0], ydev[0]), jnp.where(even, xdev[1], ydev[1]))
    return core, xdev, first, second


def rank_of(color, a, b, k):
    _, _, x, _, z, y = place()
    even = color == 0
    xx = jnp.where(even, x + a * (1 - 2 * x), x + b * (1 - 2 * x))
    yy = jnp.where(even, y + b * (1 - 2 * y), y + a * (1 - 2 * y))
    return xx * 16 + color * 8 + lax.rem(z + k, 4) * 2 + yy


def greet(devices):
    barrier = pltpu.get_barrier_semaphore()
    for device in devices:
        pl.semaphore_signal(barrier, inc=1, device_id=device, device_id_type=MESH)
    pl.semaphore_wait(barrier, len(devices))


def seq_peers(dp, sq, count):
    return [(dp, lax.rem(sq + k, count)) for k in range(1, count)]


def remote(src, dst, send, recv, device):
    return pltpu.make_async_remote_copy(
        src_ref=src, dst_ref=dst, send_sem=send, recv_sem=recv, device_id=device, device_id_type=MESH
    )


def alternate(a, b, k):
    return a * 8 + b * 4 + k


def gather_steps(w_ref, d_ref, w_all, d_all, send, recv, own):
    wr, dr = w_ref.shape[0], d_ref.shape[0]
    started = []

    def blocks(rank):
        return (
            w_all.at[pl.ds(pl.multiple_of(rank * wr, 16), wr), :],
            d_all.at[pl.ds(pl.multiple_of(rank * dr, 16), dr), :],
        )

    def pair(group, target, slot, landing_slot, mine, other):
        dp, sq, _, c, z, y = place()
        core, _, first, second = partners()
        device = {"core": core, "first": first, "second": second}.get(target)
        if device is None:
            device = (dp, lax.rem(z + target, 4) * 2 + y)
        w_dst, d_dst = blocks(rank_of(1 - c if other else c, *group))
        w_src, d_src = (w_ref, d_ref) if mine else (w_dst, d_dst)
        return (
            remote(w_src, w_dst, send.at[0, slot], recv.at[0, landing_slot], device),
            remote(d_src, d_dst, send.at[1, slot], recv.at[1, landing_slot], device),
        )

    def ship(group, target, slot, landing_slot, mine=False):
        spec = (group, target, slot, landing_slot, mine, False)
        for copy in pair(*spec):
            copy.start()
        started.append(spec)

    def arrive(group, other=False):
        for copy in pair(group, "core", 0, alternate(*group) + (16 if other else 0), False, other):
            copy.wait_recv()

    def to_core(group, mine=False):
        spot = 16 + alternate(*group)
        ship(group, "core", spot, spot, mine)

    def own_copies():
        _, _, _, c, _, _ = place()
        w_own, d_own = blocks(rank_of(c, 0, 0, 0))
        return (
            pltpu.make_async_copy(w_ref, w_own, own.at[0]),
            pltpu.make_async_copy(d_ref, d_own, own.at[1]),
        )

    def begin():
        mine = (0, 0, 0)
        ship(mine, "second", 15, 8, mine=True)
        ship(mine, "first", 3, 4, mine=True)
        for k in (1, 3, 2):
            ship(mine, k, k - 1, 4 - k, mine=True)
        to_core(mine, mine=True)
        for copy in own_copies():
            copy.start()

    def along(k):
        group = (0, 0, k)
        arrive(group)
        ship(group, "second", 8 + k - 1, 8 + k)
        ship(group, "first", 4 + k - 1, 4 + k)
        to_core(group)

    def across(k):
        group = (0, 1, k)
        arrive(group)
        ship(group, "second", 11 + k, 12 + k)
        to_core(group)

    def over(k):
        for b in (0, 1):
            group = (1, b, k)
            arrive(group)
            to_core(group)

    def finish():
        for k in (0, 1, 3, 2):
            for a, b in ((0, 0), (0, 1), (1, 0), (1, 1)):
                arrive((a, b, k), other=True)
        for copy in own_copies():
            copy.wait()
        for spec in started:
            for copy in pair(*spec):
                copy.wait_send()

    return begin, along, across, over, finish


def meeting(count):
    dp, sq, *_ = place()
    core, xdev, _, _ = partners()
    greet(seq_peers(dp, sq, count) + [core, xdev])


def tree_scratch():
    return [
        pltpu.SemaphoreType.DMA((2, 32)),
        pltpu.SemaphoreType.DMA((2, 32)),
        pltpu.SemaphoreType.DMA((2,)),
    ]


def gather_kernel(w_ref, d_ref, f_ref, w_all, d_all, f_all, send, recv, own, row_send, row_recv, row_own):
    meeting(f_ref.shape[0])
    begin, along, across, over, finish = gather_steps(w_ref, d_ref, w_all, d_all, send, recv, own)
    begin()
    rows_begin(f_ref, f_all, row_send, row_recv, row_own)
    across(0)
    along(1)
    across(1)
    over(0)
    along(3)
    across(3)
    over(1)
    along(2)
    across(2)
    over(3)
    over(2)
    finish()
    rows_end(f_ref, f_all, row_send, row_recv, row_own)


def gathered(w, d):
    return [
        jax.ShapeDtypeStruct((w.shape[0] * 32, w.shape[1]), w.dtype),
        jax.ShapeDtypeStruct((d.shape[0] * 32, d.shape[1]), d.dtype),
    ]


def gather_all(w, d, f):
    vm = pl.BlockSpec(memory_space=pltpu.VMEM)
    hbm = pl.BlockSpec(memory_space=pl.ANY)
    return pl.pallas_call(
        gather_kernel,
        in_specs=[vm] * 3,
        out_specs=[hbm] * 3,
        out_shape=gathered(w, d) + [jax.ShapeDtypeStruct(f.shape, f.dtype)],
        scratch_shapes=tree_scratch() + row_scratch(f.shape[0]),
        compiler_params=pltpu.CompilerParams(collective_id=0, has_side_effects=True),
        name="gather_all",
    )(w, d, f)


def scatter_steps(w_ref, d_ref, w_out, d_out, bufs, send, recv):
    w0, d0, w1, d1, w2, d2, w3, d3 = bufs
    wr, dr = w_out.shape[0], d_out.shape[0]

    def rows(rank, size):
        return pl.ds(pl.multiple_of(rank * size, 16), size)

    def group_rank(slot, other):
        _, _, _, c, _, _ = place()
        color = 1 - c if other else c
        return rank_of(color, lax.div(slot, 8), lax.rem(lax.div(slot, 4), 2), lax.rem(slot, 4))

    def core_copies(slot):
        core = partners()[0]
        rank = group_rank(slot, True)
        return (
            remote(w_ref.at[rows(rank, wr), :], w0.at[slot], send.at[0, slot], recv.at[0, slot], core),
            remote(d_ref.at[rows(rank, dr), :], d0.at[slot], send.at[1, slot], recv.at[1, slot], core),
        )

    def second_copies(slot):
        to = partners()[3]
        return (
            remote(w0.at[8 + slot], w1.at[slot], send.at[0, 16 + slot], recv.at[0, 16 + slot], to),
            remote(d0.at[8 + slot], d1.at[slot], send.at[1, 16 + slot], recv.at[1, 16 + slot], to),
        )

    def first_copies(slot):
        to = partners()[2]
        return (
            remote(w0.at[4 + slot], w2.at[slot], send.at[0, 24 + slot], recv.at[0, 24 + slot], to),
            remote(d0.at[4 + slot], d2.at[slot], send.at[1, 24 + slot], recv.at[1, 24 + slot], to),
        )

    def z_copies(k):
        dp, _, _, _, z, y = place()
        to = (dp, lax.rem(z + k, 4) * 2 + y)
        return (
            remote(w0.at[k], w3.at[3 - k], send.at[0, 27 + k], recv.at[0, 31 - k], to),
            remote(d0.at[k], d3.at[3 - k], send.at[1, 27 + k], recv.at[1, 31 - k], to),
        )

    def start(copies):
        for copy in copies:
            copy.start()

    def landed(copies):
        for copy in copies:
            copy.wait_recv()

    def sent(copies):
        for copy in copies:
            copy.wait_send()

    def add(slot, w, d):
        f = jnp.float32
        w0[slot] = (w0[slot].astype(f) + w.astype(f)).astype(jnp.bfloat16)
        d0[slot] = (d0[slot].astype(f) + d.astype(f)).astype(jnp.bfloat16)

    def begin():
        @pl.loop(0, 16)
        def _(step):
            start(core_copies(15 - step))

    def take(slot):
        landed(core_copies(slot))
        rank = group_rank(slot, False)
        add(slot, w_ref[rows(rank, wr), :], d_ref[rows(rank, dr), :])

    def far(lo, hi):
        @pl.loop(lo, hi)
        def _(step):
            take(15 - step)
            start(second_copies(7 - step))

    def near(lo, hi):
        @pl.loop(lo, hi)
        def _(step):
            take(7 - step)

    def pass_first(lo, hi):
        @pl.loop(lo, hi)
        def _(step):
            slot = 7 - step
            landed(second_copies(slot))
            add(slot, w1[slot], d1[slot])
            start(first_copies(slot - 4))

    def join_second():
        @pl.loop(0, 3)
        def _(step):
            slot = 3 - step
            landed(second_copies(slot))
            add(slot, w1[slot], d1[slot])

    def pass_along(lo, hi):
        @pl.loop(lo, hi)
        def _(step):
            slot = 3 - step
            landed(first_copies(slot))
            add(slot, w2[slot], d2[slot])
            start(z_copies(slot))

    def total(base, parts):
        value = base.astype(jnp.float32)
        for part in parts:
            value = value + part.astype(jnp.float32)
        return value

    def finish():
        landed(second_copies(0))
        landed(first_copies(0))
        for k in (1, 2, 3):
            landed(z_copies(k))
        w_out[...] = total(w0[0], (w1[0], w2[0], w3[0], w3[1], w3[2]))
        d_out[...] = total(d0[0], (d1[0], d2[0], d3[0], d3[1], d3[2]))

        @pl.loop(0, 16)
        def _(slot):
            sent(core_copies(slot))

        @pl.loop(0, 8)
        def _(slot):
            sent(second_copies(slot))

        @pl.loop(0, 4)
        def _(slot):
            sent(first_copies(slot))

        for k in (1, 2, 3):
            sent(z_copies(k))

    return begin, far, near, pass_first, join_second, pass_along, finish


def scatter_scratch(w, d):
    bf = jnp.bfloat16
    scratch = []
    for n in (16, 8, 4, 3):
        scratch += [
            pltpu.VMEM((n, w.shape[0] // 32, w.shape[1]), bf),
            pltpu.VMEM((n, d.shape[0] // 32, d.shape[1]), bf),
        ]
    return scratch + tree_scratch()[:2]


def scattered(w, d):
    return [
        jax.ShapeDtypeStruct((w.shape[0] // 32, w.shape[1]), jnp.float32),
        jax.ShapeDtypeStruct((d.shape[0] // 32, d.shape[1]), jnp.float32),
    ]


def scatter_kernel(w_ref, d_ref, g_ref, w_out, d_out, g_all, *scratch):
    bufs, (send, recv, row_send, row_recv, row_own) = scratch[:8], scratch[8:]
    meeting(g_ref.shape[0])
    begin, far, near, pass_first, join_second, pass_along, finish = scatter_steps(
        w_ref, d_ref, w_out, d_out, bufs, send, recv
    )
    begin()
    far(0, 8)
    rows_begin(g_ref, g_all, row_send, row_recv, row_own)
    near(0, 4)
    pass_first(0, 4)
    near(4, 8)
    join_second()
    pass_along(0, 3)
    finish()
    rows_end(g_ref, g_all, row_send, row_recv, row_own)


def scatter_all(w, d, g):
    vm = pl.BlockSpec(memory_space=pltpu.VMEM)
    hbm = pl.BlockSpec(memory_space=pl.ANY)
    return pl.pallas_call(
        scatter_kernel,
        in_specs=[vm] * 3,
        out_specs=[vm, vm, hbm],
        out_shape=scattered(w, d) + [jax.ShapeDtypeStruct(g.shape, g.dtype)],
        scratch_shapes=scatter_scratch(w, d) + row_scratch(g.shape[0]),
        compiler_params=pltpu.CompilerParams(
            collective_id=1, has_side_effects=True, vmem_limit_bytes=VMEM_LIMIT
        ),
        name="scatter_all",
    )(w, d, g)


def rows_begin(src, dst, send, recv, own):
    _, sq, *_ = place()
    for k in range(1, dst.shape[0]):
        row_copy(src, dst, send, recv, k).start()
    pltpu.make_async_copy(src.at[sq], dst.at[sq], own).start()


def rows_end(src, dst, send, recv, own):
    dp, sq, *_ = place()
    count = dst.shape[0]
    for k in range(1, count):
        copy = row_copy(src, dst, send, recv, k)
        copy.wait_send()
        landing(src, dst, send, recv, k).wait_recv()
    pltpu.make_async_copy(src.at[sq], dst.at[sq], own).wait()


def row_copy(src, dst, send, recv, k):
    dp, sq, *_ = place()
    count = dst.shape[0]
    to = lax.rem(sq + k, count)
    return remote(src.at[to], dst.at[sq], send.at[k - 1], recv.at[count - 1 - k], (dp, to))


def landing(src, dst, send, recv, k):
    dp, sq, *_ = place()
    origin = lax.rem(sq + k, dst.shape[0])
    return remote(src.at[sq], dst.at[origin], send.at[k - 1], recv.at[k - 1], (dp, origin))


def norm_parts(rows):
    centred = rows - jnp.mean(rows, axis=1, keepdims=True)
    return centred, lax.rsqrt(jnp.mean(centred * centred, axis=1, keepdims=True) + 1e-05)


def norm(rows, gain, shift):
    centred, inv = norm_parts(rows)
    return centred * inv * gain + shift


def silu(h):
    return h * (1.0 / (1.0 + jnp.exp(-h)))


def front_kernel(
    len_ref, f_ref, in_ref, pos_ref, up_ref, small_ref, down_ref, table_ref, c_ref, w_ref, d_ref,
    ctx_ref, p_ref, x1_ref, qu_ref, qv_ref, k_ref, v_ref, t_ref, sm_ref, c_all, w_all, d_all,
    send, recv, own, row_send, row_recv, row_own, *, tq, tile,
):
    low = jnp.bfloat16
    keys, model = f_ref.shape
    span = keys + tq
    steps = keys // tq
    begin, along, across, over, finish = gather_steps(w_ref, d_ref, w_all, d_all, send, recv, own)

    def dense(i):
        rows = pl.ds(pl.multiple_of(i * tile, tile), tile)
        x0 = f_ref[rows, :].astype(jnp.float32)
        a0 = norm(x0, sm_ref[0:1, :], sm_ref[6:7, :]).astype(low)
        z = silu(dotf(a0, up_ref[...])).astype(low)
        x1 = x0 + 0.5 * dotf(z, down_ref[...])
        x1_ref[rows, :] = x1
        a1 = norm(x1, sm_ref[1:2, :], sm_ref[7:8, :]).astype(low)
        query = dotf(a1, in_ref[:, :model])
        qu_ref[rows, :] = (query + sm_ref[12:13, :]).astype(low)
        qv_ref[rows, :] = (query + sm_ref[13:14, :]).astype(low)
        k_ref[rows, :] = dotf(a1, in_ref[:, model : 2 * model]).astype(low)
        v_ref[rows, :] = dotf(a1, in_ref[:, 2 * model :]).astype(low)

    @pl.when(pl.program_id(0) == 0)
    def _():
        meeting(c_ref.shape[0])
        begin()
        rows_begin(c_ref, c_all, row_send, row_recv, row_own)
        sm_ref[...] = small_ref[...].astype(jnp.float32).T

        @pl.loop(0, 2 * keys // tile)
        def _(i):
            rows = pl.ds(pl.multiple_of(i * tile, tile), tile)
            t_ref[rows, :] = dotf(table_ref[rows, :], pos_ref[...]).astype(low)

        @pl.loop(0, keys // tile)
        def _(i):
            dense(i)

            @pl.when(i == 0)
            def _():
                across(0)
                along(1)

            @pl.when(i == 1)
            def _():
                along(3)
                across(1)

            @pl.when(i == 2)
            def _():
                along(2)

    plan = {1: ((across, 3), (over, 0)), 3: ((across, 2),), 5: ((over, 1),), 8: ((over, 3),), 11: ((over, 2),)}
    dp, sq, *_ = place()
    valid = lax.broadcasted_iota(jnp.int32, (1, keys), 1) < len_ref[dp * (MB * UTTS) + sq]
    base = pl.program_id(0) * 128

    @pl.loop(0, steps)
    def _(i):
        time = pl.program_id(0) * steps + i
        for at, todo in plan.items():

            @pl.when(time == at)
            def _():
                for step, k in todo:
                    step(k)

        rows = pl.ds(pl.multiple_of(i * tq, tq), tq)
        band = pl.ds(pl.multiple_of(keys - tq - i * tq, tq), span)
        pair = pl.ds(pl.multiple_of(base, 128), 128)
        qu, qv, k, v, t = qu_ref[rows, pair], qv_ref[rows, pair], k_ref[:, pair], v_ref[:, pair], t_ref[band, pair]
        for h in range(2):
            cols = slice(h * DH, (h + 1) * DH)
            content = dotf(qu[:, cols], k[:, cols], NT)
            raw = dotf(qv[:, cols], t[:, cols], NT)
            pos = pltpu.roll(raw, keys + 1, 1, stride=1, stride_axis=0)[:, :keys]
            s = jnp.where(valid, (content + pos) * 0.125, -1e30)
            e = jnp.exp(s - jnp.max(s, axis=1, keepdims=True))
            p = (e * (1.0 / jnp.sum(e, axis=1, keepdims=True))).astype(low)
            p_ref[h, rows, :] = p
            ctx_ref[rows, cols] = dotf(p, v[:, cols]).astype(low)

    @pl.when(pl.program_id(0) == pl.num_programs(0) - 1)
    def _():
        finish()
        rows_end(c_ref, c_all, row_send, row_recv, row_own)


def row_scratch(count):
    return [
        pltpu.SemaphoreType.DMA((count - 1,)),
        pltpu.SemaphoreType.DMA((count - 1,)),
        pltpu.SemaphoreType.DMA,
    ]


def front(length, f, w_early, cuts, down, table_in, cot, w, d, tq=256, tile=256):
    rows, model = f.shape
    low = jnp.bfloat16
    vm = pl.BlockSpec(memory_space=pltpu.VMEM)
    hbm = pl.BlockSpec(memory_space=pl.ANY)

    def window(lo, hi):
        return pl.BlockSpec((w_early.shape[0], hi - lo), lambda h, *_: (0, lo // (hi - lo)), pipeline_mode=pl.Buffered(1))

    one = jax.ShapeDtypeStruct((rows, model), low)
    return pl.pallas_call(
        lambda *refs: front_kernel(*refs, tq=tq, tile=tile),
        grid_spec=pltpu.PrefetchScalarGridSpec(
            num_scalar_prefetch=1,
            grid=(model // 128,),
            in_specs=[vm] + [window(lo, hi) for lo, hi in zip(cuts[:-1], cuts[1:])] + [vm] * 5,
            out_specs=[
                pl.BlockSpec((rows, 128), lambda h, *_: (0, h)),
                pl.BlockSpec((2, rows, rows), lambda h, *_: (h, 0, 0)),
            ]
            + [vm] * 7
            + [hbm] * 3,
            scratch_shapes=tree_scratch() + row_scratch(cot.shape[0]),
        ),
        out_shape=[
            one,
            jax.ShapeDtypeStruct((model // DH, rows, rows), low),
            jax.ShapeDtypeStruct((rows, model), jnp.float32),
            one,
            one,
            one,
            one,
            jax.ShapeDtypeStruct((2 * rows, model), low),
            jax.ShapeDtypeStruct((SMALL, model), jnp.float32),
            jax.ShapeDtypeStruct(cot.shape, cot.dtype),
        ]
        + gathered(w, d),
        compiler_params=pltpu.CompilerParams(
            collective_id=4, has_side_effects=True, vmem_limit_bytes=VMEM_LIMIT
        ),
        name="front",
    )(length, f, *[w_early] * (len(cuts) - 1), down, table_in, cot, w, d)


def norm_back(rows, gain, grad):
    centred, inv = norm_parts(rows)
    hat = centred * inv
    scaled = grad * gain
    inner = jnp.mean(scaled * hat, axis=1, keepdims=True)
    out = inv * (scaled - jnp.mean(scaled, axis=1, keepdims=True) - hat * inner)
    return out, hat, jnp.sum(grad * hat, axis=0, keepdims=True)


def back_kernel(
    p_ref, g_ref, qu_ref, qv_ref, k_ref, v_ref, t_ref,
    m_ref, w_ref, d_ref, x1_ref, f_ref, grad_ref, sm_ref, gs_ref, in_ref, up_ref, down_ref, table_ref,
    ge_ref, gd_ref, rows_ref, m_all, w_out, d_out,
    ds_sc, dt_sc, dproj_sc, dtab_sc, z_sc, dh_sc, a0_sc, a1_sc, go_sc, gs_sc, *scratch, tq, tile,
):
    bufs, (send, recv, row_send, row_recv, row_own) = scratch[:8], scratch[8:]
    begin, far, near, pass_first, join_second, pass_along, finish = scatter_steps(
        w_ref, d_ref, w_out, d_out, bufs, send, recv
    )
    low = jnp.bfloat16
    keys = k_ref.shape[0]
    model = f_ref.shape[1]
    span = keys + tq
    steps = keys // tq

    def open_up():
        meeting(m_ref.shape[0])
        begin()
        gs_sc[...] = gs_ref[...]

    def rows_away():
        near(4, 8)
        rows_begin(m_ref, m_all, row_send, row_recv, row_own)

    plan = {
        0: open_up,
        1: lambda: far(0, 4),
        2: lambda: far(4, 8),
        3: lambda: near(0, 4),
        4: rows_away,
        5: lambda: pass_first(0, 2),
        6: lambda: pass_first(2, 4),
        9: join_second,
        10: lambda: pass_along(0, 2),
        11: lambda: pass_along(2, 3),
    }
    flip = (
        lax.broadcasted_iota(jnp.int32, (tq, tq), 0) + lax.broadcasted_iota(jnp.int32, (tq, tq), 1) == tq - 1
    ).astype(low)
    pad = jnp.zeros((tq, tq), jnp.float32)
    dt_sc[...] = jnp.zeros_like(dt_sc)
    base = pl.program_id(0) * 128

    def at(offset):
        return pl.ds(pl.multiple_of(base + offset, 128), 128)

    @pl.loop(0, steps)
    def _(i):
        time = pl.program_id(0) * steps + i
        for moment, step in plan.items():
            pl.when(time == moment)(step)
        rows = pl.ds(pl.multiple_of(i * tq, tq), tq)
        band = pl.ds(pl.multiple_of(keys - tq - i * tq, tq), span)
        sides = []
        for h in range(2):
            cols = slice(h * DH, (h + 1) * DH)
            dp = dotf(g_ref[rows, cols], v_ref[:, cols], NT)
            pf = p_ref[h, rows, :].astype(jnp.float32)
            ds = (pf * (dp - jnp.sum(dp * pf, axis=1, keepdims=True))).astype(low)
            ds_sc[h, rows, :] = ds
            dqu = dotf(ds, k_ref[:, cols]) * 0.125
            turned = jnp.concatenate([dotf(flip, ds), pad], axis=1)
            raw = pltpu.roll(turned, 0, 1, stride=1, stride_axis=0).astype(low)
            dqv = dotf(flip, dotf(raw, t_ref[band, cols]).astype(low)) * 0.125
            qv = dotf(flip, qv_ref[rows, cols]).astype(low)
            dt_sc[h, band, :] += dotf(raw, qv, TN)
            sides.append((dqu, dqv))
        dqu, dqv = (jnp.concatenate(both, axis=1) for both in zip(*sides))
        gs_sc[12:13, at(0)] += jnp.sum(dqu, axis=0, keepdims=True)
        gs_sc[13:14, at(0)] += jnp.sum(dqv, axis=0, keepdims=True)
        dproj_sc[rows, at(0)] = (dqu + dqv).astype(low)

    halves = []
    for h in range(2):
        cols = slice(h * DH, (h + 1) * DH)
        halves.append(
            (
                dt_sc[h] * 0.125,
                dotf(ds_sc[h], qu_ref[:, cols], TN) * 0.125,
                dotf(p_ref[h], g_ref[:, cols], TN),
            )
        )
    dtab, dk, dv = (jnp.concatenate(both, axis=1).astype(low) for both in zip(*halves))
    dtab_sc[:, at(0)] = dtab
    dproj_sc[:, at(model)] = dk
    dproj_sc[:, at(2 * model)] = dv

    @pl.when(pl.program_id(0) == pl.num_programs(0) - 1)
    def _():
        @pl.loop(0, keys // tile)
        def _(i):
            rows = pl.ds(pl.multiple_of(i * tile, tile), tile)
            dn = dotf(dproj_sc[rows, :], in_ref[...], NT)
            dx, hat, dgain = norm_back(x1_ref[rows, :], sm_ref[1:2, :], dn)
            gs_sc[1:2, :] += dgain
            gs_sc[7:8, :] += jnp.sum(dn, axis=0, keepdims=True)
            a1_sc[rows, :] = (hat * sm_ref[1:2, :] + sm_ref[7:8, :]).astype(low)
            grad = grad_ref[rows, :] + dx
            go = (0.5 * grad).astype(low)
            go_sc[rows, :] = go
            x0 = f_ref[rows, :].astype(jnp.float32)
            a0 = norm(x0, sm_ref[0:1, :], sm_ref[6:7, :]).astype(low)
            a0_sc[rows, :] = a0
            h = dotf(a0, up_ref[...])
            sig = 1.0 / (1.0 + jnp.exp(-h))
            z_sc[rows, :] = (h * sig).astype(low)
            dh = (dotf(go, down_ref[...], NT) * (sig * (1.0 + h * (1.0 - sig)))).astype(low)
            dh_sc[rows, :] = dh
            dn = dotf(dh, up_ref[...], NT)
            dx, _, dgain = norm_back(x0, sm_ref[0:1, :], dn)
            gs_sc[0:1, :] += dgain
            gs_sc[6:7, :] += jnp.sum(dn, axis=0, keepdims=True)
            rows_ref[rows, :] = (grad + dx).astype(low)

        width = model

        @pl.loop(0, 3)
        def _(j):
            cols = pl.ds(pl.multiple_of(j * width, width), width)
            ge_ref[:, cols] = dotf(a1_sc[...], dproj_sc[:, cols], TN).astype(low)

        ge_ref[:, 3 * width : 4 * width] = dotf(table_ref[...], dtab_sc[...], TN).astype(low)

        @pl.loop(0, 4)
        def _(j):
            cols = pl.ds(pl.multiple_of(j * width, width), width)
            ge_ref[:, pl.ds(pl.multiple_of((j + 4) * width, width), width)] = dotf(
                a0_sc[...], dh_sc[:, cols], TN
            ).astype(low)
            gd_ref[cols, :] = dotf(z_sc[:, cols], go_sc[...], TN).astype(low)

        ge_ref[:, 8 * width :] = gs_sc[...].T.astype(low)
        finish()
        rows_end(m_ref, m_all, row_send, row_recv, row_own)


def back(
    p, g, qu, qv, k, v, table, mixed, w, d, x1, f, grad, small, g_small, w_early, cuts, down, table_in, tq=256, tile=256
):
    rows, model = qu.shape
    low = jnp.bfloat16
    vm = pl.BlockSpec(memory_space=pltpu.VMEM)
    blk = pl.BlockSpec((rows, 128), lambda h: (0, h))
    tab = pl.BlockSpec((2 * rows, 128), lambda h: (0, h))

    def window(j):
        lo, hi = cuts[j], cuts[j + 1]
        return pl.BlockSpec((w_early.shape[0], hi - lo), lambda h: (0, lo // (hi - lo)), pipeline_mode=pl.Buffered(1))

    hidden = down.shape[0]
    return pl.pallas_call(
        lambda *refs: back_kernel(*refs, tq=tq, tile=tile),
        grid=(model // 128,),
        in_specs=[pl.BlockSpec((2, rows, rows), lambda h: (h, 0, 0))]
        + [blk] * 5
        + [tab]
        + [vm] * 8
        + [window(0), window(2), vm, vm],
        out_specs=[vm] * 3 + [pl.BlockSpec(memory_space=pl.ANY), vm, vm],
        out_shape=[
            jax.ShapeDtypeStruct(w_early.shape, low),
            jax.ShapeDtypeStruct(down.shape, low),
            jax.ShapeDtypeStruct((rows, model), low),
            jax.ShapeDtypeStruct(mixed.shape, mixed.dtype),
        ]
        + scattered(w, d),
        scratch_shapes=[
            pltpu.VMEM((2, rows, rows), low),
            pltpu.VMEM((2, 2 * rows, DH), jnp.float32),
            pltpu.VMEM((rows, 3 * model), low),
            pltpu.VMEM((2 * rows, model), low),
            pltpu.VMEM((rows, hidden), low),
            pltpu.VMEM((rows, hidden), low),
            pltpu.VMEM((rows, model), low),
            pltpu.VMEM((rows, model), low),
            pltpu.VMEM((rows, model), low),
            pltpu.VMEM((SMALL, model), jnp.float32),
        ]
        + scatter_scratch(w, d)
        + row_scratch(mixed.shape[0]),
        compiler_params=pltpu.CompilerParams(
            collective_id=5, has_side_effects=True, vmem_limit_bytes=63 * 1024 * 1024
        ),
        name="back",
    )(p, g, qu, qv, k, v, table, mixed, w, d, x1, f, grad, small, g_small, w_early, w_early, down, table_in)


def sigmoid(h):
    return 1.0 / (1.0 + jnp.exp(-h))


def middle_kernel(
    len_ref, ctx_ref, x1_ref, w_ref, down_ref, cot_ref, sm_ref,
    mixed_ref, grad_ref, gctx_ref, gw_ref, gd_ref, gs_ref,
    x2_sc, a2_sc, gate_sc, gl_sc, dep_sc, act_sc, a3_sc, z_sc, dh_sc, go_sc, gob_sc, e_sc, dd_sc, tap_sc, win_sc,
    part_sc, peer_sc, send, recv, *, tile, taps,
):
    low = jnp.bfloat16
    f32 = jnp.float32
    length, model = x1_ref.shape
    hidden = down_ref.shape[0]
    reach = (taps - 1) // 2
    edge = gl_sc.shape[0] - length
    half = edge // 2
    dp, sq, *_ = place()
    batch = lax.div(sq, UTTS)
    me = dp * UTTS + lax.rem(sq, UTTS)
    size = peer_sc.shape[1]
    valid = len_ref[dp * (MB * UTTS) + sq]
    frames = jnp.int32(0)
    for group in range(4):
        for u in range(UTTS):
            frames = frames + len_ref[group * (MB * UTTS) + batch * UTTS + u]
    per = 1.0 / jnp.full((1, model), frames, jnp.int32).astype(f32)
    up_w = w_ref.at[:, :hidden]
    out_w = w_ref.at[:, hidden : hidden + model]
    gate_w = w_ref.at[:, hidden + model : hidden + 3 * model]
    conv_w = w_ref.at[:, hidden + 3 * model :]

    def peer(j):
        r = lax.rem(me + j, size)
        return (lax.div(r, UTTS), batch * UTTS + lax.rem(r, UTTS))

    barrier = pltpu.get_barrier_semaphore()
    for j in range(1, size):
        pl.semaphore_signal(barrier, inc=1, device_id=peer(j), device_id_type=MESH)

    def give(which, j):
        return remote(
            part_sc.at[which], peer_sc.at[which, me], send.at[which, j - 1], recv.at[which, size - 1 - j], peer(j)
        )

    def give_all(which):
        for j in range(1, size):
            give(which, j).start()
        peer_sc[which, me] = part_sc[which]

    def take_all(which):
        for j in range(1, size):
            remote(
                part_sc.at[which],
                peer_sc.at[which, lax.rem(me + j, size)],
                send.at[which, j - 1],
                recv.at[which, j - 1],
                peer(j),
            ).wait_recv()
        for j in range(1, size):
            give(which, j).wait_send()
        return jnp.sum(peer_sc[which], axis=0)

    def row_of(i):
        return pl.ds(pl.multiple_of(i * tile, tile), tile)

    def inner_of(i):
        return pl.ds(pl.multiple_of(i * tile + half, 8), tile)

    def mask_of(i):
        return (lax.broadcasted_iota(jnp.int32, (tile, 1), 0) + i * tile < valid).astype(f32)

    def total(rows):
        return jnp.sum(rows, axis=0, keepdims=True)

    def row(r):
        return sm_ref[r : r + 1, :]

    gs_ref[...] = jnp.zeros_like(gs_ref)
    part_sc[...] = jnp.zeros_like(part_sc)
    for pad_sc in (gl_sc, dd_sc):
        pad_sc[:half, :] = jnp.zeros((half, model), f32)
        pad_sc[half + length :, :] = jnp.zeros((half, model), f32)

    tiles = length // tile

    @pl.loop(0, tiles)
    def _(i):
        rows = row_of(i)
        x2 = x1_ref[rows, :] + dotf(ctx_ref[rows, :], out_w[...])
        x2_sc[rows, :] = x2
        a2 = norm(x2, row(2), row(8)).astype(low)
        a2_sc[rows, :] = a2
        gate = dotf(a2, gate_w[...])
        gate_sc[rows, :] = gate
        gl = (gate[:, :model] * sigmoid(gate[:, model:]) * mask_of(i)).astype(low)
        gl_sc[inner_of(i), :] = gl.astype(f32)

    strip = STRIP

    def depthwise(src, lanes, base, backward):
        win_sc[...] = src[pl.ds(base, strip + edge), lanes]
        acc = jnp.zeros((strip, 128), f32)
        for k in range(taps):
            shift = half + (reach - k if backward else k - reach)
            acc = acc + win_sc[shift : shift + strip, :] * sm_ref[14 + k : 15 + k, lanes]
        return acc

    for c in range(model // 128):
        lanes = slice(c * 128, (c + 1) * 128)

        @pl.loop(0, length // strip)
        def _(i):
            base = pl.multiple_of(i * strip, strip)
            dep = depthwise(gl_sc, lanes, base, False)
            dep_sc[pl.ds(base, strip), lanes] = dep
            mask = (lax.broadcasted_iota(jnp.int32, (strip, 1), 0) + base < valid).astype(f32)
            kept = dep * mask
            part_sc[0, 0:1, lanes] += total(kept)
            part_sc[0, 1:2, lanes] += total(kept * dep)

    pl.semaphore_wait(barrier, size - 1)
    give_all(0)
    sums = take_all(0)
    mean = sums[0:1] * per
    inv = lax.rsqrt(sums[1:2] * per - mean * mean + 1e-05)

    @pl.loop(0, tiles)
    def _(i):
        rows = row_of(i)
        dep = dep_sc[rows, :]
        hatn = (dep - mean) * inv
        normal = hatn * row(5) + row(11)
        sgn = sigmoid(normal)
        act = (normal * sgn).astype(low)
        act_sc[rows, :] = act
        x3 = x2_sc[rows, :] + dotf(act, conv_w[...])
        a3 = norm(x3, row(3), row(9)).astype(low)
        a3_sc[rows, :] = a3
        h = dotf(a3, up_w[...])
        sig = sigmoid(h)
        z = (h * sig).astype(low)
        z_sc[rows, :] = z
        x4 = x3 + 0.5 * dotf(z, down_ref[...])
        mixed_ref[rows, :] = norm(x4, row(4), row(10)).astype(low)
        cot = cot_ref[rows, :].astype(f32)
        grad, _, dgain = norm_back(x4, row(4), cot)
        gs_ref[4:5, :] += dgain
        gs_ref[10:11, :] += total(cot)
        go = (0.5 * grad).astype(low)
        go_sc[rows, :] = go
        dh = (dotf(go, down_ref[...], NT) * (sig * (1.0 + h * (1.0 - sig)))).astype(low)
        dh_sc[rows, :] = dh
        dn = dotf(dh, up_w[...], NT)
        dx, _, dgain = norm_back(x3, row(3), dn)
        gs_ref[3:4, :] += dgain
        gs_ref[9:10, :] += total(dn)
        grad = grad + dx
        grad_ref[rows, :] = grad
        gob = grad.astype(low)
        gob_sc[rows, :] = gob
        dnormal = dotf(gob, conv_w[...], NT) * (sgn * (1.0 + normal * (1.0 - sgn)))
        gs_ref[5:6, :] += total(dnormal * hatn)
        gs_ref[11:12, :] += total(dnormal)
        e = dnormal * row(5)
        e_sc[rows, :] = e
        part_sc[1, 0:1, :] += total(e)
        part_sc[1, 1:2, :] += total(e * dep)

    give_all(1)

    @pl.loop(0, hidden // model)
    def _(j):
        cols = pl.ds(pl.multiple_of(j * model, model), model)
        gw_ref[:, cols] = dotf(a3_sc[...], dh_sc[:, cols], TN).astype(low)
        gd_ref[cols, :] = dotf(z_sc[:, cols], go_sc[...], TN).astype(low)

    gw_ref[:, hidden + 3 * model :] = dotf(act_sc[...], gob_sc[...], TN).astype(low)
    sums = take_all(1)
    dvar = -0.5 * inv * inv * inv * (sums[1:2] - mean * sums[0:1])
    dmean = -inv * sums[0:1] - 2.0 * mean * dvar

    @pl.loop(0, tiles)
    def _(i):
        rows = row_of(i)
        dd = e_sc[rows, :] * inv + mask_of(i) * (dmean * per + 2.0 * dep_sc[rows, :] * dvar * per)
        dd_sc[inner_of(i), :] = dd.astype(low).astype(f32)

    for c in range(model // 128):
        lanes = slice(c * 128, (c + 1) * 128)
        tap_sc[...] = jnp.zeros_like(tap_sc)

        @pl.loop(0, length // strip)
        def _(i):
            base = pl.multiple_of(i * strip, strip)
            e_sc[pl.ds(base, strip), lanes] = depthwise(dd_sc, lanes, base, True)
            dd = dd_sc[pl.ds(pl.multiple_of(base + half, 8), strip), lanes]
            win_sc[...] = gl_sc[pl.ds(base, strip + edge), lanes]
            for k in range(taps):
                prod = win_sc[half + k - reach : half + k - reach + strip, :] * dd
                tap_sc[k] += jnp.sum(prod.reshape(strip // 8, 8, 128), axis=0)

        gs_ref[14 : 14 + taps, lanes] = jnp.sum(tap_sc[...], axis=1)

    @pl.loop(0, tiles)
    def _(i):
        rows = row_of(i)
        dgl = e_sc[rows, :] * mask_of(i)
        ga = gate_sc[rows, :model]
        sb = sigmoid(gate_sc[rows, model:])
        dgate = jnp.concatenate([dgl * sb, dgl * ga * sb * (1.0 - sb)], axis=1).astype(low)
        dh_sc[rows, : 2 * model] = dgate
        dn = dotf(dgate, gate_w[...], NT)
        dx, _, dgain = norm_back(x2_sc[rows, :], row(2), dn)
        gs_ref[2:3, :] += dgain
        gs_ref[8:9, :] += total(dn)
        grad = grad_ref[rows, :] + dx
        grad_ref[rows, :] = grad
        gob = grad.astype(low)
        gob_sc[rows, :] = gob
        gctx_ref[rows, :] = dotf(gob, out_w[...], NT).astype(low)

    gw_ref[:, hidden + model : hidden + 3 * model] = dotf(a2_sc[...], dh_sc[:, : 2 * model], TN).astype(low)
    gw_ref[:, hidden : hidden + model] = dotf(ctx_ref[...], gob_sc[...], TN).astype(low)


def middle(lengths, ctx, x1, w, down, cot, small, taps, tile=256):
    rows, model = x1.shape
    hidden = down.shape[0]
    low = jnp.bfloat16
    f32 = jnp.float32
    vm = pl.BlockSpec(memory_space=pltpu.VMEM)
    size = 4 * UTTS
    half = -(-(taps - 1) // 2 // 8) * 8
    wide = pltpu.VMEM((rows, model), f32)
    thin = pltpu.VMEM((rows, model), low)
    padded = pltpu.VMEM((rows + 2 * half, model), f32)
    return pl.pallas_call(
        lambda *refs: middle_kernel(*refs, tile=tile, taps=taps),
        in_specs=[pl.BlockSpec(memory_space=pltpu.SMEM)] + [vm] * 6,
        out_specs=[vm] * 6,
        out_shape=[
            jax.ShapeDtypeStruct((rows, model), low),
            jax.ShapeDtypeStruct((rows, model), f32),
            jax.ShapeDtypeStruct((rows, model), low),
            jax.ShapeDtypeStruct(w.shape, low),
            jax.ShapeDtypeStruct(down.shape, low),
            jax.ShapeDtypeStruct((SMALL, model), f32),
        ],
        scratch_shapes=[
            wide,
            thin,
            pltpu.VMEM((rows, 2 * model), f32),
            padded,
            wide,
            thin,
            thin,
            pltpu.VMEM((rows, hidden), low),
            pltpu.VMEM((rows, hidden), low),
            thin,
            thin,
            wide,
            padded,
            pltpu.VMEM((taps, 8, 128), f32),
            pltpu.VMEM((STRIP + 2 * half, 128), f32),
            pltpu.VMEM((2, 2, model), f32),
            pltpu.VMEM((2, size, 2, model), f32),
            pltpu.SemaphoreType.DMA((2, size - 1)),
            pltpu.SemaphoreType.DMA((2, size - 1)),
        ],
        compiler_params=pltpu.CompilerParams(
            collective_id=2, has_side_effects=True, vmem_limit_bytes=63 * 1024 * 1024
        ),
        name="middle",
    )(lengths, ctx, x1, w, down, cot, small)


def position_table(length, width):
    offsets = (length - 1 - np.arange(2 * length)).astype(np.float32)
    half = width // 2
    steps = np.arange(half, dtype=np.float32) * np.float32(-2.0 * math.log(10000.0) / width)
    angles = (offsets[:, None] * np.exp(steps)[None, :]).astype(np.float64)
    table = np.concatenate([np.sin(angles), np.cos(angles)], axis=1)
    return jnp.asarray(table.astype(np.float32)).astype(jnp.bfloat16)


def columns(*members):
    return [0] + [int(v) for v in np.cumsum([member.shape[1] for member in members])]


def split(values, cuts):
    return [values[:, lo:hi] for lo, hi in zip(cuts[:-1], cuts[1:])]


def local_whole(
    frames,
    lengths,
    cotangent,
    gains,
    shifts,
    rel_bias,
    ffn_up,
    ffn_down,
    attn_in,
    attn_out,
    pos_proj,
    conv_in,
    depthwise,
    conv_out,
):
    low = jnp.bfloat16
    _, width_rows, model = frames.shape
    length = width_rows * lax.axis_size("seq")
    taps = depthwise.shape[2]
    small = jnp.concatenate([gains[0], shifts[0], rel_bias[0]], axis=0).T
    small = jnp.concatenate([small, depthwise[0]], axis=1)
    small = jnp.pad(small, ((0, 0), (0, SMALL - small.shape[1])))
    early = jnp.concatenate([attn_in[0], pos_proj[0], ffn_up[0, 0], small], axis=1)
    late = jnp.concatenate([ffn_up[0, 1], attn_out[0], conv_in[0], conv_out[0]], axis=1)
    cuts_early = columns(attn_in[0], pos_proj[0], ffn_up[0, 0], small)
    cuts_late = columns(ffn_up[0, 1], attn_out[0], conv_in[0], conv_out[0])
    w_early, down_0, f_all = gather_all(early, ffn_down[0, 0], frames.astype(low))
    table_in = position_table(length, model)

    ctx, probs, x1, qu, qv, key, value, table, small, c_all, w_late, down_1 = front(
        lengths,
        f_all.reshape(length, model),
        w_early,
        cuts_early,
        down_0,
        table_in,
        cotangent.astype(low),
        late,
        ffn_down[0, 1],
    )
    mixed, grad, grad_ctx, g_late, g_down1, g_small = middle(
        lengths, ctx, x1, w_late, down_1, c_all.reshape(length, model), small, taps
    )
    g_early, g_down0, grad, m_all, late_sum, down1_sum = back(
        probs,
        grad_ctx,
        qu,
        qv,
        key,
        value,
        table,
        mixed.reshape(frames.shape),
        g_late,
        g_down1,
        x1,
        f_all.reshape(length, model),
        grad,
        small,
        g_small,
        w_early,
        cuts_early,
        down_0,
        table_in,
    )
    early_sum, down0_sum, g_all = scatter_all(g_early, g_down0, grad.reshape(frames.shape))
    s_attn_in, s_pos, s_up0, tail = split(early_sum, cuts_early)
    s_up1, s_attn_out, s_conv_in, s_conv_out = split(late_sum, cuts_late)
    rows = tail[:, :14].T
    return (
        m_all.astype(jnp.float32),
        g_all.astype(jnp.float32),
        rows[None, 0:6],
        rows[None, 6:12],
        rows[None, 12:14],
        jnp.stack([s_up0, s_up1])[None],
        jnp.stack([down0_sum, down1_sum])[None],
        s_attn_in[None],
        s_attn_out[None],
        s_pos[None],
        s_conv_in[None],
        tail[None, :, 14 : 14 + taps],
        s_conv_out[None],
    )


def solution(mesh):
    body = local_whole if fits_whole(mesh) else local_general
    in_specs = (
        P("dp", "seq", None),
        P(),
        P("dp", "seq", None),
        P(None, None, ("dp", "seq")),
        P(None, None, ("dp", "seq")),
        P(None, None, ("dp", "seq")),
        P(None, None, ("dp", "seq"), None),
        P(None, None, ("dp", "seq"), None),
        P(None, ("dp", "seq"), None),
        P(None, ("dp", "seq"), None),
        P(None, ("dp", "seq"), None),
        P(None, ("dp", "seq"), None),
        P(None, ("dp", "seq"), None),
        P(None, ("dp", "seq"), None),
    )
    out_specs = (
        P("dp", "seq", None),
        P("dp", "seq", None),
        P(None, None, ("dp", "seq")),
        P(None, None, ("dp", "seq")),
        P(None, None, ("dp", "seq")),
        P(None, None, ("dp", "seq"), None),
        P(None, None, ("dp", "seq"), None),
        P(None, ("dp", "seq"), None),
        P(None, ("dp", "seq"), None),
        P(None, ("dp", "seq"), None),
        P(None, ("dp", "seq"), None),
        P(None, ("dp", "seq"), None),
        P(None, ("dp", "seq"), None),
    )
    return jax.shard_map(body, mesh=mesh, in_specs=in_specs, out_specs=out_specs, check_vma=False)
```

profile of v0, /device:TPU:1, one launch (start us, length us, event | category | flops | bytes accessed | tf_op | source)
XLA Modules:
  0.0 317.8 jit_solution(18190506686615296583)
XLA Ops:
  0.6 0.0 copy-start
  0.7 0.9 copy.28
  1.5 0.8 copy.29
  2.3 0.7 copy.30
  3.1 0.1 maximum_bitcast_fusion.2
  3.1 0.8 fusion.2
  3.9 0.9 slice_bitcast_fusion.5
  4.8 1.4 pad_maximum_fusion.1.refs_9_
  6.2 1.5 pad_maximum_fusion.w_ref
  7.7 1.5 slice_bitcast_fusion.4
  9.2 2.4 convert_element_type.17.f_ref
  11.6 0.0 copy-done
  11.6 1.0 convert_element_type.19.refs_8_
  12.6 49.7 %gather_all.1 = (bf16[512,4224]{1,0:T(8,128)(2,1)}, bf16[2048,512]{1,0:T(8,128)(2,1)}, bf16[8,96,512]{2,1,0:T(8,128)(2,1)}) custom-call(bf16[16,4224]{1,0:T(8,128)(2,1)} %pad_maximum_fusion.w_ref, bf16[64,512]{1,0:T(8,128)(2,1)} %get-tuple-element.89.d_ref, bf16[8,96,512]{2,1,0:T(8,128)(2,1)} %convert_element_type.17.f_ref), custom_call_target="tpu_custom_call" | custom-call | tf_op jit(solution)/shard_map/gather_all/pallas_call | solution.py:840
  62.3 68.2 %front.1 = (bf16[768,512]{1,0:T(8,128)(2,1)}, bf16[8,768,768]{2,1,0:T(8,128)(2,1)}, f32[768,512]{1,0:T(8,128)}, bf16[768,512]{1,0:T(8,128)(2,1)}, bf16[768,512]{...) custom-call(s32[32]{0:T(128)} %refs_0_.3, ...), custom_call_target="tpu_custom_call" | custom-call | tf_op jit(solution)/shard_map/front/pallas_call | solution.py:1191
  130.6 48.6 %middle.1 = (bf16[768,512]{1,0:T(8,128)(2,1)}, f32[768,512]{1,0:T(8,128)}, bf16[768,512]{1,0:T(8,128)(2,1)}, bf16[512,4096]{1,0:T(8,128)(2,1)}, bf16[2048,512]{1,0:T(8,128)(2,1)}, /*index=5*/f32[128,512]{1,0:T(8,128)}) custom-call(s32[32]{0:T(128)} %refs_0_.3, bf16[768,512]{1,0:T(8,128)(2,1)} %get-tuple-element.47.refs_1_, ...), custom_call_target="tpu_custom_call" | custom-call | tf_op jit(solution)/shard_map/middle/pallas_call | solution.py:1659
  179.2 69.1 %back.1 = (bf16[512,4224]{1,0:T(8,128)(2,1)}, bf16[2048,512]{1,0:T(8,128)(2,1)}, bf16[768,512]{1,0:T(8,128)(2,1)}, bf16[8,96,512]{2,1,0:T(8,128)(2,1)}, f32[16,4096]{1,0:T(8,128)}, /*index=5*/f32[64,512]{1,0:T(8,128)}) custom-call(bf16[8,768,768]{2,1,0:T(8,128)(2,1)} %get-tuple-element.46.refs_0_, bf16[768,512]{1,0:T(8,128)(2,1)} %get-tuple-element.53.refs_1_, ...), custom_call_target="tpu_custom_call" | custom-call | tf_op jit(solution)/shard_map/back/pallas_call | solution.py:1385
  248.3 1.5 slice_bitcast_fusion.3
  249.7 2.5 convert_element_type.20
  252.2 0.0 copy-start.3
  252.2 0.0 copy-start.2
  252.2 53.8 %scatter_all.1 = (f32[16,4224]{1,0:T(8,128)}, f32[64,512]{1,0:T(8,128)}, bf16[8,96,512]{2,1,0:T(8,128)(2,1)}) custom-call(bf16[512,4224]{1,0:T(8,128)(2,1)} %get-tuple-element.65.w_ref, bf16[2048,512]{1,0:T(8,128)(2,1)} %get-tuple-element.66.d_ref, bf16[8,96,512]{2,1,0:T(8,128)(2,1)} %bitcast.54), custom_call_target="tpu_custom_call" | custom-call | tf_op jit(solution)/shard_map/scatter_all/pallas_call | solution.py:1025
  306.0 0.0 copy-start.1
  306.0 0.0 copy-done.3
  306.0 1.7 maximum_bitcast_fusion.1
  307.7 0.7 slice_bitcast_fusion.14
  308.4 0.1 slice.69
  308.5 0.6 copy.33
  309.2 1.4 slice_bitcast_fusion.13
  310.5 0.1 slice_bitcast_fusion.11
  310.6 0.7 copy.35
  311.2 0.7 copy.34
  311.9 1.5 slice_bitcast_fusion.2
  313.4 0.0 copy-done.2
  313.4 1.4 slice_bitcast_fusion.8
  314.8 0.9 slice_bitcast_fusion
  315.8 0.7 maximum_bitcast_fusion
  316.5 0.0 copy-done.1
  316.5 1.4 convert_element_type.21
Async XLA Ops:
  0.6 11.0 %copy-start = (f32[8,96,512]{2,1,0:T(8,128)S(1)}, f32[8,96,512]{2,1,0:T(8,128)}, u32[]{:S(2)}) copy-start(f32[8,96,512]{2,1,0:T(8,128)} %param.17) | copy-start | bytes 4718596
  252.2 53.8 %copy-start.3 = (f32[64,512]{1,0:T(8,128)S(1)}, f32[64,512]{1,0:T(8,128)}, u32[]{:S(2)}) copy-start(f32[64,512]{1,0:T(8,128)} %get-tuple-element.72) | copy-start | bytes 393220
  252.2 61.2 %copy-start.2 = (f32[16,4096]{1,0:T(8,128)S(1)}, f32[16,4096]{1,0:T(8,128)}, u32[]{:S(2)}) copy-start(f32[16,4096]{1,0:T(8,128)} %get-tuple-element.70) | copy-start | bytes 786436
  306.0 10.5 %copy-start.1 = (bf16[8,96,512]{2,1,0:T(8,128)(2,1)S(1)}, bf16[8,96,512]{2,1,0:T(8,128)(2,1)}, u32[]{:S(2)}) copy-start(bf16[8,96,512]{2,1,0:T(8,128)(2,1)} %get-tuple-element.68) | copy-start | bytes 2359300
where the time goes:
time: 319 us; the launch traced here: 318 us
  Pallas kernels  289 us (91%)
  local copies, waits for them, and re-layouts  14.3 us (4%)
  other arithmetic  13.4 us (4%)
    pallas_call x1, Pallas kernels, back(): pl.pallas_call(lambda *refs: back_kernel(*refs, tq=tq, tile=tile), grid=(...  69.1 us
    pallas_call x1, Pallas kernels, front(): pl.pallas_call(lambda *refs: front_kernel(*refs, tq=tq, tile=tile), grid_...  68.2 us
    pallas_call x1, Pallas kernels, scatter_all(): pl.pallas_call(scatter_kernel, in_specs=[vm] * 3, out_specs=[vm, vm, hbm]...  53.8 us
    pallas_call x1, Pallas kernels, gather_all(): pl.pallas_call(gather_kernel, in_specs=[vm] * 3, out_specs=[hbm] * 3, out...  49.7 us
    pallas_call x1, Pallas kernels, middle(): pl.pallas_call(lambda *refs: middle_kernel(*refs, tile=tile, taps=taps),...  48.6 us

commit v1 on v0

--- a/solution.py
+++ b/solution.py
@@ -674,12 +674,12 @@
     ydev = (dp, z * 2 + 1 - y)
     first = (jnp.where(even, ydev[0], xdev[0]), jnp.where(even, ydev[1], xdev[1]))
     second = (jnp.where(even, xdev[0], ydev[0]), jnp.where(even, xdev[1], ydev[1]))
-    return core, xdev, first, second
-
-
-def rank_of(color, a, b, k):
+    return core, xdev, first, second, ydev
+
+
+def rank_of(color, a, b, k, fixed=False):
     _, _, x, _, z, y = place()
-    even = color == 0
+    even = jnp.logical_or(color == 0, fixed)
     xx = jnp.where(even, x + a * (1 - 2 * x), x + b * (1 - 2 * x))
     yy = jnp.where(even, y + b * (1 - 2 * y), y + a * (1 - 2 * y))
     return xx * 16 + color * 8 + lax.rem(z + k, 4) * 2 + yy
@@ -710,23 +710,24 @@
     wr, dr = w_ref.shape[0], d_ref.shape[0]
     started = []
 
-    def blocks(rank):
+    def blocks(w_rank, d_rank):
         return (
-            w_all.at[pl.ds(pl.multiple_of(rank * wr, 16), wr), :],
-            d_all.at[pl.ds(pl.multiple_of(rank * dr, 16), dr), :],
+            w_all.at[pl.ds(pl.multiple_of(w_rank * wr, 16), wr), :],
+            d_all.at[pl.ds(pl.multiple_of(d_rank * dr, 16), dr), :],
         )
 
     def pair(group, target, slot, landing_slot, mine, other):
         dp, sq, _, c, z, y = place()
-        core, _, first, second = partners()
-        device = {"core": core, "first": first, "second": second}.get(target)
-        if device is None:
-            device = (dp, lax.rem(z + target, 4) * 2 + y)
-        w_dst, d_dst = blocks(rank_of(1 - c if other else c, *group))
+        core, xdev, first, second, ydev = partners()
+        along_z = (dp, lax.rem(z + target, 4) * 2 + y) if isinstance(target, int) else None
+        w_to = {"core": core, "first": first, "second": second}.get(target, along_z)
+        d_to = {"core": core, "first": ydev, "second": xdev}.get(target, along_z)
+        color = 1 - c if other else c
+        w_dst, d_dst = blocks(rank_of(color, *group), rank_of(color, *group, fixed=True))
         w_src, d_src = (w_ref, d_ref) if mine else (w_dst, d_dst)
         return (
-            remote(w_src, w_dst, send.at[0, slot], recv.at[0, landing_slot], device),
-            remote(d_src, d_dst, send.at[1, slot], recv.at[1, landing_slot], device),
+            remote(w_src, w_dst, send.at[0, slot], recv.at[0, landing_slot], w_to),
+            remote(d_src, d_dst, send.at[1, slot], recv.at[1, landing_slot], d_to),
         )
 
     def ship(group, target, slot, landing_slot, mine=False):
@@ -745,7 +746,8 @@
 
     def own_copies():
         _, _, _, c, _, _ = place()
-        w_own, d_own = blocks(rank_of(c, 0, 0, 0))
+        mine = rank_of(c, 0, 0, 0)
+        w_own, d_own = blocks(mine, mine)
         return (
             pltpu.make_async_copy(w_ref, w_own, own.at[0]),
             pltpu.make_async_copy(d_ref, d_own, own.at[1]),
@@ -795,7 +797,7 @@
 
 def meeting(count):
     dp, sq, *_ = place()
-    core, xdev, _, _ = partners()
+    core, xdev, *_ = partners()
     greet(seq_peers(dp, sq, count) + [core, xdev])
 
 
@@ -811,16 +813,16 @@
     meeting(f_ref.shape[0])
     begin, along, across, over, finish = gather_steps(w_ref, d_ref, w_all, d_all, send, recv, own)
     begin()
-    rows_begin(f_ref, f_all, row_send, row_recv, row_own)
     across(0)
     along(1)
+    along(3)
     across(1)
+    along(2)
+    rows_begin(f_ref, f_all, row_send, row_recv, row_own)
+    across(3)
     over(0)
-    along(3)
-    across(3)
+    across(2)
     over(1)
-    along(2)
-    across(2)
     over(3)
     over(2)
     finish()
@@ -855,31 +857,31 @@
     def rows(rank, size):
         return pl.ds(pl.multiple_of(rank * size, 16), size)
 
-    def group_rank(slot, other):
+    def group_ranks(slot, other):
         _, _, _, c, _, _ = place()
-        color = 1 - c if other else c
-        return rank_of(color, lax.div(slot, 8), lax.rem(lax.div(slot, 4), 2), lax.rem(slot, 4))
+        group = (1 - c if other else c, lax.div(slot, 8), lax.rem(lax.div(slot, 4), 2), lax.rem(slot, 4))
+        return rank_of(*group), rank_of(*group, fixed=True)
 
     def core_copies(slot):
         core = partners()[0]
-        rank = group_rank(slot, True)
+        w_rank, d_rank = group_ranks(slot, True)
         return (
-            remote(w_ref.at[rows(rank, wr), :], w0.at[slot], send.at[0, slot], recv.at[0, slot], core),
-            remote(d_ref.at[rows(rank, dr), :], d0.at[slot], send.at[1, slot], recv.at[1, slot], core),
+            remote(w_ref.at[rows(w_rank, wr), :], w0.at[slot], send.at[0, slot], recv.at[0, slot], core),
+            remote(d_ref.at[rows(d_rank, dr), :], d0.at[slot], send.at[1, slot], recv.at[1, slot], core),
         )
 
     def second_copies(slot):
-        to = partners()[3]
+        _, xdev, _, to, _ = partners()
         return (
             remote(w0.at[8 + slot], w1.at[slot], send.at[0, 16 + slot], recv.at[0, 16 + slot], to),
-            remote(d0.at[8 + slot], d1.at[slot], send.at[1, 16 + slot], recv.at[1, 16 + slot], to),
+            remote(d0.at[8 + slot], d1.at[slot], send.at[1, 16 + slot], recv.at[1, 16 + slot], xdev),
         )
 
     def first_copies(slot):
-        to = partners()[2]
+        _, _, to, _, ydev = partners()
         return (
             remote(w0.at[4 + slot], w2.at[slot], send.at[0, 24 + slot], recv.at[0, 24 + slot], to),
-            remote(d0.at[4 + slot], d2.at[slot], send.at[1, 24 + slot], recv.at[1, 24 + slot], to),
+            remote(d0.at[4 + slot], d2.at[slot], send.at[1, 24 + slot], recv.at[1, 24 + slot], ydev),
         )
 
     def z_copies(k):
@@ -914,8 +916,8 @@
 
     def take(slot):
         landed(core_copies(slot))
-        rank = group_rank(slot, False)
-        add(slot, w_ref[rows(rank, wr), :], d_ref[rows(rank, dr), :])
+        w_rank, d_rank = group_ranks(slot, False)
+        add(slot, w_ref[rows(w_rank, wr), :], d_ref[rows(d_rank, dr), :])
 
     def far(lo, hi):
         @pl.loop(lo, hi)
@@ -1108,7 +1110,6 @@
     def _():
         meeting(c_ref.shape[0])
         begin()
-        rows_begin(c_ref, c_all, row_send, row_recv, row_own)
         sm_ref[...] = small_ref[...].astype(jnp.float32).T
 
         @pl.loop(0, 2 * keys // tile)
@@ -1133,6 +1134,7 @@
             @pl.when(i == 2)
             def _():
                 along(2)
+                rows_begin(c_ref, c_all, row_send, row_recv, row_own)
 
     plan = {1: ((across, 3), (over, 0)), 3: ((across, 2),), 5: ((over, 1),), 8: ((over, 3),), 11: ((over, 2),)}
     dp, sq, *_ = place()
@@ -1705,12 +1707,97 @@
     return jnp.asarray(table.astype(np.float32)).astype(jnp.bfloat16)
 
 
-def columns(*members):
-    return [0] + [int(v) for v in np.cumsum([member.shape[1] for member in members])]
-
-
-def split(values, cuts):
-    return [values[:, lo:hi] for lo, hi in zip(cuts[:-1], cuts[1:])]
+def pack_kernel(
+    frames, cot, gains, shifts, rel, up, down, attn_in, attn_out, pos, conv_in, taps, conv_out,
+    early, late, down_0, down_1, f_out, c_out, turn, table,
+):
+    low = jnp.bfloat16
+    f32 = jnp.float32
+    own = gains.shape[2]
+    count = taps.shape[2]
+    at = 0
+    for piece in (attn_in[0], pos[0], up[0, 0]):
+        early[:, at : at + piece.shape[1]] = piece
+        at += piece.shape[1]
+    table[...] = jnp.zeros_like(table)
+    turn[...] = jnp.zeros_like(turn)
+    turn[:own, :count] = taps[0].astype(f32)
+    table[0:6, :own] = gains[0].astype(f32)
+    table[6:12, :own] = shifts[0].astype(f32)
+    table[12:14, :own] = rel[0].astype(f32)
+    table[14 : 14 + count, :own] = turn[...].T[:count, :own]
+    early[:, at:] = table[...].T[:own, :].astype(low)
+    at = 0
+    for piece in (up[0, 1], attn_out[0], conv_in[0], conv_out[0]):
+        late[:, at : at + piece.shape[1]] = piece
+        at += piece.shape[1]
+    down_0[...] = down[0, 0]
+    down_1[...] = down[0, 1]
+    f_out[...] = frames[...].astype(low)
+    c_out[...] = cot[...].astype(low)
+
+
+def pack(frames, cot, *weights):
+    low = jnp.bfloat16
+    vm = pl.BlockSpec(memory_space=pltpu.VMEM)
+    _, _, _, up, down, attn_in, attn_out, pos, conv_in, _, conv_out = weights
+    own = attn_in.shape[1]
+    early = attn_in.shape[2] + pos.shape[2] + up.shape[3] + SMALL
+    late = up.shape[3] + attn_out.shape[2] + conv_in.shape[2] + conv_out.shape[2]
+    shapes = [(own, early), (own, late), down.shape[2:], down.shape[2:], frames.shape, frames.shape]
+    return pl.pallas_call(
+        pack_kernel,
+        in_specs=[vm] * 13,
+        out_specs=[vm] * 6,
+        out_shape=[jax.ShapeDtypeStruct(shape, low) for shape in shapes],
+        scratch_shapes=[pltpu.VMEM((SMALL, SMALL), jnp.float32)] * 2,
+        name="pack",
+    )(frames, cot, *weights)
+
+
+def unpack_kernel(
+    early, late, down_0, down_1, m_rows, g_rows,
+    mixed, grad, gains, shifts, rel, up, down, attn_in, attn_out, pos, conv_in, taps, conv_out, turn, table,
+):
+    f32 = jnp.float32
+    own = early.shape[0]
+    count = taps.shape[2]
+    at = 0
+    for piece in (attn_in, pos):
+        piece[0] = early[:, at : at + piece.shape[2]]
+        at += piece.shape[2]
+    up[0, 0] = early[:, at : at + up.shape[3]]
+    at += up.shape[3]
+    turn[...] = jnp.zeros_like(turn)
+    turn[:own, :] = early[:, at:]
+    table[...] = turn[...].T
+    gains[0] = table[0:6, :own]
+    shifts[0] = table[6:12, :own]
+    rel[0] = table[12:14, :own]
+    turn[:count, :] = table[14 : 14 + count, :]
+    taps[0] = turn[...].T[:own, :count]
+    up[0, 1] = late[:, : up.shape[3]]
+    at = up.shape[3]
+    for piece in (attn_out, conv_in, conv_out):
+        piece[0] = late[:, at : at + piece.shape[2]]
+        at += piece.shape[2]
+    down[0, 0] = down_0[...]
+    down[0, 1] = down_1[...]
+    mixed[...] = m_rows[...].astype(f32)
+    grad[...] = g_rows[...].astype(f32)
+
+
+def unpack(early, late, down_0, down_1, m_rows, g_rows, likes):
+    vm = pl.BlockSpec(memory_space=pltpu.VMEM)
+    shapes = [m_rows.shape, g_rows.shape] + [like.shape for like in likes]
+    return pl.pallas_call(
+        unpack_kernel,
+        in_specs=[vm] * 6,
+        out_specs=[vm] * 13,
+        out_shape=[jax.ShapeDtypeStruct(shape, jnp.float32) for shape in shapes],
+        scratch_shapes=[pltpu.VMEM((SMALL, SMALL), jnp.float32)] * 2,
+        name="unpack",
+    )(early, late, down_0, down_1, m_rows, g_rows)
 
 
 def local_whole(
@@ -1729,30 +1816,20 @@
     depthwise,
     conv_out,
 ):
-    low = jnp.bfloat16
+    weights = (
+        gains, shifts, rel_bias, ffn_up, ffn_down, attn_in, attn_out, pos_proj, conv_in, depthwise, conv_out
+    )
     _, width_rows, model = frames.shape
     length = width_rows * lax.axis_size("seq")
     taps = depthwise.shape[2]
-    small = jnp.concatenate([gains[0], shifts[0], rel_bias[0]], axis=0).T
-    small = jnp.concatenate([small, depthwise[0]], axis=1)
-    small = jnp.pad(small, ((0, 0), (0, SMALL - small.shape[1])))
-    early = jnp.concatenate([attn_in[0], pos_proj[0], ffn_up[0, 0], small], axis=1)
-    late = jnp.concatenate([ffn_up[0, 1], attn_out[0], conv_in[0], conv_out[0]], axis=1)
-    cuts_early = columns(attn_in[0], pos_proj[0], ffn_up[0, 0], small)
-    cuts_late = columns(ffn_up[0, 1], attn_out[0], conv_in[0], conv_out[0])
-    w_early, down_0, f_all = gather_all(early, ffn_down[0, 0], frames.astype(low))
     table_in = position_table(length, model)
-
+    early, late, own_0, own_1, f_rows, c_rows = pack(frames, cotangent, *weights)
+    sizes = (attn_in.shape[2], pos_proj.shape[2], ffn_up.shape[3], SMALL)
+    cuts = [0] + [int(v) for v in np.cumsum(sizes)]
+    w_early, down_0, f_all = gather_all(early, own_0, f_rows)
+    f_all = f_all.reshape(length, model)
     ctx, probs, x1, qu, qv, key, value, table, small, c_all, w_late, down_1 = front(
-        lengths,
-        f_all.reshape(length, model),
-        w_early,
-        cuts_early,
-        down_0,
-        table_in,
-        cotangent.astype(low),
-        late,
-        ffn_down[0, 1],
+        lengths, f_all, w_early, cuts, down_0, table_in, c_rows, late, own_1
     )
     mixed, grad, grad_ctx, g_late, g_down1, g_small = middle(
         lengths, ctx, x1, w_late, down_1, c_all.reshape(length, model), small, taps
@@ -1769,34 +1846,17 @@
         g_late,
         g_down1,
         x1,
-        f_all.reshape(length, model),
+        f_all,
         grad,
         small,
         g_small,
         w_early,
-        cuts_early,
+        cuts,
         down_0,
         table_in,
     )
     early_sum, down0_sum, g_all = scatter_all(g_early, g_down0, grad.reshape(frames.shape))
-    s_attn_in, s_pos, s_up0, tail = split(early_sum, cuts_early)
-    s_up1, s_attn_out, s_conv_in, s_conv_out = split(late_sum, cuts_late)
-    rows = tail[:, :14].T
-    return (
-        m_all.astype(jnp.float32),
-        g_all.astype(jnp.float32),
-        rows[None, 0:6],
-        rows[None, 6:12],
-        rows[None, 12:14],
-        jnp.stack([s_up0, s_up1])[None],
-        jnp.stack([down0_sum, down1_sum])[None],
-        s_attn_in[None],
-        s_attn_out[None],
-        s_pos[None],
-        s_conv_in[None],
-        tail[None, :, 14 : 14 + taps],
-        s_conv_out[None],
-    )
+    return tuple(unpack(early_sum, late_sum, down0_sum, down1_sum, m_all, g_all, weights))
 
 
 def solution(mesh):

time: 319 us -> 296 us (0.928)
  other arithmetic: 13.4 us -> 0 us
  local copies, waits for them, and re-layouts: 14.3 us -> 2.51 us
    convert_element_type x4 -> x0, other arithmetic: 7.21 us -> none  [the longest x1 2.49 us: local_whole(): m_all.astype(jnp.float32)]
    pallas_call x0 -> x2, Pallas kernels: none -> 7.2 us  [the longest x1 3.77 us: unpack(): pl.pallas_call(unpack_kernel, in_specs=[vm] * 6, out_specs=[vm] * 13, out...]
    broadcast_in_dim x5 -> x0, local copies, waits for them, and re-layouts: 5.85 us -> none  [the longest x1 1.54 us: local_whole(): s_attn_in[None]]
    squeeze x5 -> x0, local copies, waits for them, and re-layouts: 4.81 us -> none  [the longest x3 2.4 us: local_whole(): small = jnp.concatenate([gains[0], shifts[0], rel_bias[0]], axis=0).T]
    pallas_call x1, Pallas kernels: 53.8 us -> 57.9 us  [scatter_all(): pl.pallas_call(scatter_kernel, in_specs=[vm] * 3, out_specs=[vm, vm, hbm]...]
    pallas_call x1, Pallas kernels: 68.2 us -> 64.3 us  [front(): pl.pallas_call(lambda *refs: front_kernel(*refs, tq=tq, tile=tile), grid_...]
    concatenate x3 -> x0, other arithmetic: 3.69 us -> none  [the longest x1 1.48 us: local_whole(): jnp.concatenate([attn_in[0], pos_proj[0], ffn_up[0, 0], small], axis=1)]
where the time goes in v1:
time: 296 us; the launch traced here: 295 us
  Pallas kernels  292 us (99%)
    pallas_call x1, Pallas kernels, back(): pl.pallas_call(lambda *refs: back_kernel(*refs, tq=tq, tile=tile), grid=(...  68.8 us
    pallas_call x1, Pallas kernels, front(): pl.pallas_call(lambda *refs: front_kernel(*refs, tq=tq, tile=tile), grid_...  64.3 us
    pallas_call x1, Pallas kernels, scatter_all(): pl.pallas_call(scatter_kernel, in_specs=[vm] * 3, out_specs=[vm, vm, hbm]...  57.9 us
    pallas_call x1, Pallas kernels, gather_all(): pl.pallas_call(gather_kernel, in_specs=[vm] * 3, out_specs=[hbm] * 3, out...  47.4 us
    pallas_call x1, Pallas kernels, middle(): pl.pallas_call(lambda *refs: middle_kernel(*refs, tile=tile, taps=taps),...  46.6 us

profile of v1, /device:TPU:1, one launch (start us, length us, event | category | flops | bytes accessed | tf_op | source)
XLA Modules:
  0.0 295.5 jit_solution(11483463974951865957)
XLA Ops:
  0.6 3.4 %pack.1 = (bf16[16,4224]{1,0:T(8,128)(2,1)}, bf16[16,4096]{1,0:T(8,128)(2,1)}, bf16[64,512]{1,0:T(8,128)(2,1)}, bf16[64,512]{1,0:T(8,128)(2,1)}, bf16[8,96,512]{...) custom-call(f32[8,96,512]{2,1,0:T(8,128)} %frames.1, f32[8,96,512]{2,1,0:T(8,128)} %cot.1, bf16[1,6,16]{2,1,0:T(8,128)(2,1)} %gains.1, ...), custom_call_target="tpu_custom_call" | custom-call | tf_op jit(solution)/shard_map/pack/pallas_call | solution.py:1748
  4.1 47.4 %gather_all.1 = (bf16[512,4224]{1,0:T(8,128)(2,1)}, bf16[2048,512]{1,0:T(8,128)(2,1)}, bf16[8,96,512]{2,1,0:T(8,128)(2,1)}) custom-call(bf16[16,4224]{1,0:T(8,128)(2,1)} %get-tuple-element.49.w_ref, bf16[64,512]{1,0:T(8,128)(2,1)} %get-tuple-element.50.d_ref, bf16[8,96,512]{2,1,0:T(8,128)(2,1)} %get-tuple-element.51.f_ref), custom_call_target="tpu_custom_call" | custom-call | tf_op jit(solution)/shard_map/gather_all/pallas_call | solution.py:842
  51.5 64.3 %front.1 = (bf16[768,512]{1,0:T(8,128)(2,1)}, bf16[8,768,768]{2,1,0:T(8,128)(2,1)}, f32[768,512]{1,0:T(8,128)}, bf16[768,512]{1,0:T(8,128)(2,1)}, bf16[768,512]{...) custom-call(s32[32]{0:T(128)} %refs_0_.3, ...), custom_call_target="tpu_custom_call" | custom-call | tf_op jit(solution)/shard_map/front/pallas_call | solution.py:1193
  115.8 46.6 %middle.1 = (bf16[768,512]{1,0:T(8,128)(2,1)}, f32[768,512]{1,0:T(8,128)}, bf16[768,512]{1,0:T(8,128)(2,1)}, bf16[512,4096]{1,0:T(8,128)(2,1)}, bf16[2048,512]{1,0:T(8,128)(2,1)}, /*index=5*/f32[128,512]{1,0:T(8,128)}) custom-call(s32[32]{0:T(128)} %refs_0_.3, bf16[768,512]{1,0:T(8,128)(2,1)} %get-tuple-element.59.refs_1_, ...), custom_call_target="tpu_custom_call" | custom-call | tf_op jit(solution)/shard_map/middle/pallas_call | solution.py:1661
  162.4 68.8 %back.1 = (bf16[512,4224]{1,0:T(8,128)(2,1)}, bf16[2048,512]{1,0:T(8,128)(2,1)}, bf16[768,512]{1,0:T(8,128)(2,1)}, bf16[8,96,512]{2,1,0:T(8,128)(2,1)}, f32[16,4096]{1,0:T(8,128)}, /*index=5*/f32[64,512]{1,0:T(8,128)}) custom-call(bf16[8,768,768]{2,1,0:T(8,128)(2,1)} %get-tuple-element.58.refs_0_, bf16[768,512]{1,0:T(8,128)(2,1)} %get-tuple-element.65.refs_1_, ...), custom_call_target="tpu_custom_call" | custom-call | tf_op jit(solution)/shard_map/back/pallas_call | solution.py:1387
  231.3 57.9 %scatter_all.1 = (f32[16,4224]{1,0:T(8,128)}, f32[64,512]{1,0:T(8,128)}, bf16[8,96,512]{2,1,0:T(8,128)(2,1)}) custom-call(bf16[512,4224]{1,0:T(8,128)(2,1)} %get-tuple-element.76.w_ref, bf16[2048,512]{1,0:T(8,128)(2,1)} %get-tuple-element.77.d_ref, bf16[8,96,512]{2,1,0:T(8,128)(2,1)} %bitcast.6), custom_call_target="tpu_custom_call" | custom-call | tf_op jit(solution)/shard_map/scatter_all/pallas_call | solution.py:1027
  289.2 3.8 %unpack.1 = (f32[8,96,512]{2,1,0:T(8,128)}, f32[8,96,512]{2,1,0:T(8,128)}, f32[1,6,16]{2,1,0:T(8,128)}, f32[1,6,16]{2,1,0:T(8,128)}, f32[1,2,16]{2,1,0:T(2,128)}...) custom-call(f32[16,4224]{1,0:T(8,128)} %get-tuple-element.79.early, ...), custom_call_target="tpu_custom_call" | custom-call | tf_op jit(solution)/shard_map/unpack/pallas_call | solution.py:1793
  293.0 1.3 copy.28
  294.2 1.3 copy.29

commit v2 on v1

--- a/solution.py
+++ b/solution.py
@@ -904,54 +904,62 @@
         for copy in copies:
             copy.wait_send()
 
+    def add_to(buf, slot, more):
+        buf[slot] = (buf[slot].astype(jnp.float32) + more.astype(jnp.float32)).astype(jnp.bfloat16)
+
     def add(slot, w, d):
-        f = jnp.float32
-        w0[slot] = (w0[slot].astype(f) + w.astype(f)).astype(jnp.bfloat16)
-        d0[slot] = (d0[slot].astype(f) + d.astype(f)).astype(jnp.bfloat16)
-
-    def begin():
+        add_to(w0, slot, w)
+        add_to(d0, slot, d)
+
+    def spot_of(step):
+        return (1 - lax.rem(step, 2)) * 4 + 3 - lax.div(step, 2)
+
+    def begin(parts=(0, 1)):
         @pl.loop(0, 16)
         def _(step):
-            start(core_copies(15 - step))
-
-    def take(slot):
-        landed(core_copies(slot))
+            copies = core_copies(8 * (1 - lax.div(step, 8)) + spot_of(lax.rem(step, 8)))
+            for part in parts:
+                copies[part].start()
+
+    def take(slot, parts=(0, 1)):
+        copies = core_copies(slot)
         w_rank, d_rank = group_ranks(slot, False)
-        add(slot, w_ref[rows(w_rank, wr), :], d_ref[rows(d_rank, dr), :])
-
-    def far(lo, hi):
+        for part in parts:
+            copies[part].wait_recv()
+        if 0 in parts:
+            add_to(w0, slot, w_ref[rows(w_rank, wr), :])
+        if 1 in parts:
+            add_to(d0, slot, d_ref[rows(d_rank, dr), :])
+
+    def far(lo, hi, parts=(0, 1)):
         @pl.loop(lo, hi)
         def _(step):
-            take(15 - step)
-            start(second_copies(7 - step))
-
-    def near(lo, hi):
-        @pl.loop(lo, hi)
-        def _(step):
-            take(7 - step)
-
-    def pass_first(lo, hi):
-        @pl.loop(lo, hi)
-        def _(step):
-            slot = 7 - step
-            landed(second_copies(slot))
-            add(slot, w1[slot], d1[slot])
-            start(first_copies(slot - 4))
-
-    def join_second():
-        @pl.loop(0, 3)
-        def _(step):
-            slot = 3 - step
-            landed(second_copies(slot))
-            add(slot, w1[slot], d1[slot])
-
-    def pass_along(lo, hi):
-        @pl.loop(lo, hi)
-        def _(step):
-            slot = 3 - step
-            landed(first_copies(slot))
-            add(slot, w2[slot], d2[slot])
-            start(z_copies(slot))
+            spot = spot_of(step)
+            take(8 + spot, parts)
+            copies = second_copies(spot)
+            for part in parts:
+                copies[part].start()
+
+    def join(k):
+        take(4 + k)
+        landed(second_copies(4 + k))
+        add(4 + k, w1[4 + k], d1[4 + k])
+        start(first_copies(k))
+        take(k)
+        landed(second_copies(k))
+        add(k, w1[k], d1[k])
+
+    def onward(k):
+        landed(first_copies(k))
+        add(k, w2[k], d2[k])
+        start(z_copies(k))
+
+    def near(step):
+        join(3 - step)
+
+        @pl.when(step >= 1)
+        def _():
+            onward(4 - step)
 
     def total(base, parts):
         value = base.astype(jnp.float32)
@@ -960,12 +968,11 @@
         return value
 
     def finish():
-        landed(second_copies(0))
         landed(first_copies(0))
         for k in (1, 2, 3):
             landed(z_copies(k))
-        w_out[...] = total(w0[0], (w1[0], w2[0], w3[0], w3[1], w3[2]))
-        d_out[...] = total(d0[0], (d1[0], d2[0], d3[0], d3[1], d3[2]))
+        w_out[...] = total(w0[0], (w2[0], w3[0], w3[1], w3[2]))
+        d_out[...] = total(d0[0], (d2[0], d3[0], d3[1], d3[2]))
 
         @pl.loop(0, 16)
         def _(slot):
@@ -982,7 +989,7 @@
         for k in (1, 2, 3):
             sent(z_copies(k))
 
-    return begin, far, near, pass_first, join_second, pass_along, finish
+    return begin, far, near, finish
 
 
 def scatter_scratch(w, d):
@@ -1003,45 +1010,11 @@
     ]
 
 
-def scatter_kernel(w_ref, d_ref, g_ref, w_out, d_out, g_all, *scratch):
-    bufs, (send, recv, row_send, row_recv, row_own) = scratch[:8], scratch[8:]
-    meeting(g_ref.shape[0])
-    begin, far, near, pass_first, join_second, pass_along, finish = scatter_steps(
-        w_ref, d_ref, w_out, d_out, bufs, send, recv
-    )
-    begin()
-    far(0, 8)
-    rows_begin(g_ref, g_all, row_send, row_recv, row_own)
-    near(0, 4)
-    pass_first(0, 4)
-    near(4, 8)
-    join_second()
-    pass_along(0, 3)
-    finish()
-    rows_end(g_ref, g_all, row_send, row_recv, row_own)
-
-
-def scatter_all(w, d, g):
-    vm = pl.BlockSpec(memory_space=pltpu.VMEM)
-    hbm = pl.BlockSpec(memory_space=pl.ANY)
-    return pl.pallas_call(
-        scatter_kernel,
-        in_specs=[vm] * 3,
-        out_specs=[vm, vm, hbm],
-        out_shape=scattered(w, d) + [jax.ShapeDtypeStruct(g.shape, g.dtype)],
-        scratch_shapes=scatter_scratch(w, d) + row_scratch(g.shape[0]),
-        compiler_params=pltpu.CompilerParams(
-            collective_id=1, has_side_effects=True, vmem_limit_bytes=VMEM_LIMIT
-        ),
-        name="scatter_all",
-    )(w, d, g)
-
-
 def rows_begin(src, dst, send, recv, own):
     _, sq, *_ = place()
     for k in range(1, dst.shape[0]):
         row_copy(src, dst, send, recv, k).start()
-    pltpu.make_async_copy(src.at[sq], dst.at[sq], own).start()
+    pltpu.make_async_copy(block_of(src, sq, dst), dst.at[sq], own).start()
 
 
 def rows_end(src, dst, send, recv, own):
@@ -1051,20 +1024,25 @@
         copy = row_copy(src, dst, send, recv, k)
         copy.wait_send()
         landing(src, dst, send, recv, k).wait_recv()
-    pltpu.make_async_copy(src.at[sq], dst.at[sq], own).wait()
+    pltpu.make_async_copy(block_of(src, sq, dst), dst.at[sq], own).wait()
 
 
 def row_copy(src, dst, send, recv, k):
     dp, sq, *_ = place()
     count = dst.shape[0]
     to = lax.rem(sq + k, count)
-    return remote(src.at[to], dst.at[sq], send.at[k - 1], recv.at[count - 1 - k], (dp, to))
+    return remote(block_of(src, to, dst), dst.at[sq], send.at[k - 1], recv.at[count - 1 - k], (dp, to))
+
+
+def block_of(src, index, dst):
+    width = dst.shape[1]
+    return src.at[pl.ds(pl.multiple_of(index * width, 16), width), :] if len(src.shape) == 2 else src.at[index]
 
 
 def landing(src, dst, send, recv, k):
     dp, sq, *_ = place()
     origin = lax.rem(sq + k, dst.shape[0])
-    return remote(src.at[sq], dst.at[origin], send.at[k - 1], recv.at[k - 1], (dp, origin))
+    return remote(block_of(src, sq, dst), dst.at[origin], send.at[k - 1], recv.at[k - 1], (dp, origin))
 
 
 def norm_parts(rows):
@@ -1236,13 +1214,14 @@
 def back_kernel(
     p_ref, g_ref, qu_ref, qv_ref, k_ref, v_ref, t_ref,
     m_ref, w_ref, d_ref, x1_ref, f_ref, grad_ref, sm_ref, gs_ref, in_ref, up_ref, down_ref, table_ref,
-    ge_ref, gd_ref, rows_ref, m_all, w_out, d_out,
-    ds_sc, dt_sc, dproj_sc, dtab_sc, z_sc, dh_sc, a0_sc, a1_sc, go_sc, gs_sc, *scratch, tq, tile,
+    m_all, w_out, d_out, g_all, e_out, l_out,
+    ge_ref, gd_ref, rows_ref, ds_sc, dt_sc, dproj_sc, dtab_sc, z_sc, dh_sc, a0_sc, a1_sc, go_sc, gs_sc, *scratch, tq, tile,
 ):
-    bufs, (send, recv, row_send, row_recv, row_own) = scratch[:8], scratch[8:]
-    begin, far, near, pass_first, join_second, pass_along, finish = scatter_steps(
-        w_ref, d_ref, w_out, d_out, bufs, send, recv
-    )
+    bufs, (send, recv, send_2, recv_2), rows_m, rows_g = scratch[:8], scratch[8:12], scratch[12:15], scratch[15:]
+    wide = w_ref.shape[1]
+    trimmed = [buf.at[:, :, :wide] if j % 2 == 0 else buf for j, buf in enumerate(bufs)]
+    begin, far, near, finish = scatter_steps(w_ref, d_ref, w_out, d_out, trimmed, send, recv)
+    again = scatter_steps(ge_ref, gd_ref, e_out, l_out, bufs, send_2, recv_2)
     low = jnp.bfloat16
     keys = k_ref.shape[0]
     model = f_ref.shape[1]
@@ -1254,21 +1233,11 @@
         begin()
         gs_sc[...] = gs_ref[...]
 
-    def rows_away():
-        near(4, 8)
-        rows_begin(m_ref, m_all, row_send, row_recv, row_own)
-
     plan = {
         0: open_up,
         1: lambda: far(0, 4),
         2: lambda: far(4, 8),
-        3: lambda: near(0, 4),
-        4: rows_away,
-        5: lambda: pass_first(0, 2),
-        6: lambda: pass_first(2, 4),
-        9: join_second,
-        10: lambda: pass_along(0, 2),
-        11: lambda: pass_along(2, 3),
+        5: lambda: rows_begin(m_ref, m_all, *rows_m),
     }
     flip = (
         lax.broadcasted_iota(jnp.int32, (tq, tq), 0) + lax.broadcasted_iota(jnp.int32, (tq, tq), 1) == tq - 1
@@ -1285,6 +1254,12 @@
         time = pl.program_id(0) * steps + i
         for moment, step in plan.items():
             pl.when(time == moment)(step)
+        due = jnp.logical_and(jnp.logical_and(time >= 4, time <= 10), lax.rem(time, 2) == 0)
+
+        @pl.when(due)
+        def _():
+            near(lax.div(time, 2) - 2)
+
         rows = pl.ds(pl.multiple_of(i * tq, tq), tq)
         band = pl.ds(pl.multiple_of(keys - tq - i * tq, tq), span)
         sides = []
@@ -1348,26 +1323,40 @@
             gs_sc[6:7, :] += jnp.sum(dn, axis=0, keepdims=True)
             rows_ref[rows, :] = (grad + dx).astype(low)
 
+        rows_begin(rows_ref, g_all, *rows_g)
         width = model
+
+        def piece(j):
+            return pl.ds(pl.multiple_of(j * width, width), width)
+
+        @pl.loop(0, 4)
+        def _(j):
+            gd_ref[piece(j), :] = dotf(z_sc[:, piece(j)], go_sc[...], TN).astype(low)
+
+        finish()
+        rows_end(m_ref, m_all, *rows_m)
+        meeting(m_ref.shape[0])
+        begin_2, far_2, near_2, end = again
+        begin_2((1,))
+        far_2(0, 4, (1,))
 
         @pl.loop(0, 3)
         def _(j):
-            cols = pl.ds(pl.multiple_of(j * width, width), width)
-            ge_ref[:, cols] = dotf(a1_sc[...], dproj_sc[:, cols], TN).astype(low)
-
+            ge_ref[:, piece(j)] = dotf(a1_sc[...], dproj_sc[:, piece(j)], TN).astype(low)
+
+        far_2(4, 8, (1,))
         ge_ref[:, 3 * width : 4 * width] = dotf(table_ref[...], dtab_sc[...], TN).astype(low)
 
         @pl.loop(0, 4)
         def _(j):
-            cols = pl.ds(pl.multiple_of(j * width, width), width)
-            ge_ref[:, pl.ds(pl.multiple_of((j + 4) * width, width), width)] = dotf(
-                a0_sc[...], dh_sc[:, cols], TN
-            ).astype(low)
-            gd_ref[cols, :] = dotf(z_sc[:, cols], go_sc[...], TN).astype(low)
+            ge_ref[:, piece(j + 4)] = dotf(a0_sc[...], dh_sc[:, piece(j)], TN).astype(low)
 
         ge_ref[:, 8 * width :] = gs_sc[...].T.astype(low)
-        finish()
-        rows_end(m_ref, m_all, row_send, row_recv, row_own)
+        begin_2((0,))
+        far_2(0, 8, (0,))
+        pl.loop(0, 4)(near_2)
+        end()
+        rows_end(rows_ref, g_all, *rows_g)
 
 
 def back(
@@ -1376,6 +1365,7 @@
     rows, model = qu.shape
     low = jnp.bfloat16
     vm = pl.BlockSpec(memory_space=pltpu.VMEM)
+    hbm = pl.BlockSpec(memory_space=pl.ANY)
     blk = pl.BlockSpec((rows, 128), lambda h: (0, h))
     tab = pl.BlockSpec((2 * rows, 128), lambda h: (0, h))
 
@@ -1392,15 +1382,15 @@
         + [tab]
         + [vm] * 8
         + [window(0), window(2), vm, vm],
-        out_specs=[vm] * 3 + [pl.BlockSpec(memory_space=pl.ANY), vm, vm],
-        out_shape=[
-            jax.ShapeDtypeStruct(w_early.shape, low),
-            jax.ShapeDtypeStruct(down.shape, low),
-            jax.ShapeDtypeStruct((rows, model), low),
-            jax.ShapeDtypeStruct(mixed.shape, mixed.dtype),
-        ]
-        + scattered(w, d),
+        out_specs=[hbm, vm, vm, hbm, vm, vm],
+        out_shape=[jax.ShapeDtypeStruct(mixed.shape, low)]
+        + scattered(w, d)
+        + [jax.ShapeDtypeStruct(mixed.shape, low)]
+        + scattered(w_early, down),
         scratch_shapes=[
+            pltpu.VMEM(w_early.shape, low),
+            pltpu.VMEM(down.shape, low),
+            pltpu.VMEM((rows, model), low),
             pltpu.VMEM((2, rows, rows), low),
             pltpu.VMEM((2, 2 * rows, DH), jnp.float32),
             pltpu.VMEM((rows, 3 * model), low),
@@ -1412,7 +1402,9 @@
             pltpu.VMEM((rows, model), low),
             pltpu.VMEM((SMALL, model), jnp.float32),
         ]
-        + scatter_scratch(w, d)
+        + scatter_scratch(w_early, down)
+        + tree_scratch()[:2]
+        + row_scratch(mixed.shape[0])
         + row_scratch(mixed.shape[0]),
         compiler_params=pltpu.CompilerParams(
             collective_id=5, has_side_effects=True, vmem_limit_bytes=63 * 1024 * 1024
@@ -1834,7 +1826,7 @@
     mixed, grad, grad_ctx, g_late, g_down1, g_small = middle(
         lengths, ctx, x1, w_late, down_1, c_all.reshape(length, model), small, taps
     )
-    g_early, g_down0, grad, m_all, late_sum, down1_sum = back(
+    m_all, late_sum, down1_sum, g_all, early_sum, down0_sum = back(
         probs,
         grad_ctx,
         qu,
@@ -1855,7 +1847,6 @@
         down_0,
         table_in,
     )
-    early_sum, down0_sum, g_all = scatter_all(g_early, g_down0, grad.reshape(frames.shape))
     return tuple(unpack(early_sum, late_sum, down0_sum, down1_sum, m_all, g_all, weights))
 
 

time: 296 us -> 288 us (0.973)
  Pallas kernels: 292 us -> 284 us
    pallas_call x1 -> x0, Pallas kernels: 57.9 us -> none  [scatter_all(): pl.pallas_call(scatter_kernel, in_specs=[vm] * 3, out_specs=[vm, vm, hbm]...]
    pallas_call x1, Pallas kernels: 68.8 us -> 119 us  [back(): pl.pallas_call(lambda *refs: back_kernel(*refs, tq=tq, tile=tile), grid=(...]
where the time goes in v2:
time: 288 us
  Pallas kernels  284 us (99%)
    pallas_call x1, Pallas kernels, back(): pl.pallas_call(lambda *refs: back_kernel(*refs, tq=tq, tile=tile), grid=(...  119 us
    pallas_call x1, Pallas kernels, front(): pl.pallas_call(lambda *refs: front_kernel(*refs, tq=tq, tile=tile), grid_...  64.2 us
    pallas_call x1, Pallas kernels, gather_all(): pl.pallas_call(gather_kernel, in_specs=[vm] * 3, out_specs=[hbm] * 3, out...  47.4 us
    pallas_call x1, Pallas kernels, middle(): pl.pallas_call(lambda *refs: middle_kernel(*refs, tile=tile, taps=taps),...  46.5 us

profile of v2, /device:TPU:1, one launch (start us, length us, event | category | flops | bytes accessed | tf_op | source)
XLA Modules:
  0.0 287.6 jit_solution(7850610924685891502)
XLA Ops:
  0.6 3.4 %pack.1 = (bf16[16,4224]{1,0:T(8,128)(2,1)}, bf16[16,4096]{1,0:T(8,128)(2,1)}, bf16[64,512]{1,0:T(8,128)(2,1)}, bf16[64,512]{1,0:T(8,128)(2,1)}, bf16[8,96,512]{...) custom-call(f32[8,96,512]{2,1,0:T(8,128)} %frames.1, f32[8,96,512]{2,1,0:T(8,128)} %cot.1, bf16[1,6,16]{2,1,0:T(8,128)(2,1)} %gains.1, ...), custom_call_target="tpu_custom_call" | custom-call | tf_op jit(solution)/shard_map/pack/pallas_call | solution.py:1740
  4.1 47.4 %gather_all.1 = (bf16[512,4224]{1,0:T(8,128)(2,1)}, bf16[2048,512]{1,0:T(8,128)(2,1)}, bf16[8,96,512]{2,1,0:T(8,128)(2,1)}) custom-call(bf16[16,4224]{1,0:T(8,128)(2,1)} %get-tuple-element.46.w_ref, bf16[64,512]{1,0:T(8,128)(2,1)} %get-tuple-element.47.d_ref, bf16[8,96,512]{2,1,0:T(8,128)(2,1)} %get-tuple-element.48.f_ref), custom_call_target="tpu_custom_call" | custom-call | tf_op jit(solution)/shard_map/gather_all/pallas_call | solution.py:842
  51.5 64.2 %front.1 = (bf16[768,512]{1,0:T(8,128)(2,1)}, bf16[8,768,768]{2,1,0:T(8,128)(2,1)}, f32[768,512]{1,0:T(8,128)}, bf16[768,512]{1,0:T(8,128)(2,1)}, bf16[768,512]{...) custom-call(s32[32]{0:T(128)} %refs_0_.3, ...), custom_call_target="tpu_custom_call" | custom-call | tf_op jit(solution)/shard_map/front/pallas_call | solution.py:1171
  115.8 46.5 %middle.1 = (bf16[768,512]{1,0:T(8,128)(2,1)}, f32[768,512]{1,0:T(8,128)}, bf16[768,512]{1,0:T(8,128)(2,1)}, bf16[512,4096]{1,0:T(8,128)(2,1)}, bf16[2048,512]{1,0:T(8,128)(2,1)}, /*index=5*/f32[128,512]{1,0:T(8,128)}) custom-call(s32[32]{0:T(128)} %refs_0_.3, bf16[768,512]{1,0:T(8,128)(2,1)} %get-tuple-element.56.refs_1_, ...), custom_call_target="tpu_custom_call" | custom-call | tf_op jit(solution)/shard_map/middle/pallas_call | solution.py:1653
  162.3 119.0 %back.1 = (bf16[8,96,512]{2,1,0:T(8,128)(2,1)}, f32[16,4096]{1,0:T(8,128)}, f32[64,512]{1,0:T(8,128)}, bf16[8,96,512]{2,1,0:T(8,128)(2,1)}, f32[16,4224]{1,0:T(8,128)}, /*index=5*/f32[64,512]{1,0:T(8,128)}) custom-call(bf16[8,768,768]{2,1,0:T(8,128)(2,1)} %get-tuple-element.55.refs_0_, bf16[768,512]{1,0:T(8,128)(2,1)} %get-tuple-element.62.refs_1_, ...), custom_call_target="tpu_custom_call" | custom-call | tf_op jit(solution)/shard_map/back/pallas_call | solution.py:1377
  281.3 3.8 %unpack.1 = (f32[8,96,512]{2,1,0:T(8,128)}, f32[8,96,512]{2,1,0:T(8,128)}, f32[1,6,16]{2,1,0:T(8,128)}, f32[1,6,16]{2,1,0:T(8,128)}, f32[1,2,16]{2,1,0:T(2,128)}...) custom-call(f32[16,4224]{1,0:T(8,128)} %get-tuple-element.73.early, ...), custom_call_target="tpu_custom_call" | custom-call | tf_op jit(solution)/shard_map/unpack/pallas_call | solution.py:1785
  285.1 1.3 copy.28
  286.4 1.3 copy.29
